TPU v7x, 256 devices: a whole 4x4x8 slice. The times are simulated.
256 devices in a mesh: gx: 8 (over y, core), gy: 16 (over x_lo, z), gz: 2 (over x_hi).
Axes of the slice: x: 4 (x_hi: 2, x_lo: 2; x = x_hi * 2 + x_lo), y: 4, z: 8, core: 2. Of those that a mesh axis runs over, the one named last changes fastest.
Arguments:
- permittivity: float32 [64, 512, 256], P('gx', 'gy', 'gz'), may hold values from 1 to 9
- loss: float32 [64, 512, 256], P('gx', 'gy', 'gz'), may hold values from 0 to 0.2
- fwd_electric: float32 [3, 64, 512, 256], P(None, 'gx', 'gy', 'gz'), may hold values from -6 to 6
- fwd_magnetic: float32 [3, 64, 512, 256], P(None, 'gx', 'gy', 'gz'), may hold values from -6 to 6
- adj_electric: float32 [3, 64, 512, 256], P(None, 'gx', 'gy', 'gz'), may hold values from -200 to 200
- adj_magnetic: float32 [3, 64, 512, 256], P(None, 'gx', 'gy', 'gz'), may hold values from -200 to 200
- wavelet: float32 [64], replicated, may hold values from -6 to 6
- residuals: float32 [2048, 64], P(('gx', 'gy', 'gz')), may hold values from -24 to 24
- source_cell: int32 [1], replicated, may hold values from 0 to 8388607
- receiver_cells: int32 [2048], replicated, may hold values from 0 to 8388607
- start_step: int32 [1], replicated, may hold values from 0 to 60
Outputs:
- direction: float32 [64, 512, 256], P('gx', 'gy', 'gz')
- grad_rms: float32 [], replicated
Inputs may be any that keep to these rules, and one draw needn't show every extreme that they name: source_cell[0] is a flat index of a cell. receiver_cells[r] is the flat index of receiver r's cell; several receivers may share a cell. Samples start_step to start_step + 3 exist in every trace.
All inputs are finite; a program needn't handle non-finite values.
Results may differ from a plain program's by a relative error of at most 0.0003.
Values sent between devices are 32-bit elements; how exact they have to be, the bound alone decides.
A program may use at most 128 MiB of HBM per device.

v0:
```python
import functools

import jax
import jax.numpy as jnp
from jax import lax
from jax.sharding import Mesh
from jax.sharding import PartitionSpec as P

STEPS = 4
GX = ("gx_0", "gx_1")
GY = ("gy_0", "gy_1")
GX_GY_GZ = ("gx_0", "gx_1", "gy_0", "gy_1", "gz")


def passed_along(block, axis, distance):
    devices = range(lax.axis_size(axis))
    route = [(i - distance, i) for i in devices if i - distance in devices]
    return lax.ppermute(block, axis, route)


def edges_of(length, count):
    unit = 8 if length >= 8 * count else 1
    return [length // unit * k // count * unit for k in range(1, count)]


def all_blocks(value, axes, sequence):
    pieces = value
    for k in sequence:
        pieces = lax.all_gather(pieces, axes[k])
    done = sequence[::-1]
    back = [done.index(k) for k in range(len(axes))]
    pieces = pieces.transpose(*back, *range(len(axes), pieces.ndim))
    return pieces.reshape(-1, *value.shape)


def in_order(pieces, dim):
    shape = list(pieces.shape[1:])
    shape[dim] *= pieces.shape[0]
    return jnp.moveaxis(pieces, 0, dim).reshape(shape)


def gather_all_axes(value, axes, dim):
    numbers = list(range(len(axes)))[::-1]
    widest = value.shape.index(max(value.shape[:-1] or value.shape))
    edges = [0, *edges_of(value.shape[widest], len(axes)), value.shape[widest]]
    gathered = []
    for k, (start, end) in enumerate(zip(edges, edges[1:])):
        if end > start:
            share = lax.slice_in_dim(value, start, end, axis=widest)
            gathered.append(all_blocks(share, axes, numbers[k:] + numbers[:k]))
    return in_order(jnp.concatenate(gathered, axis=widest + 1), dim)


def by_axis(value, axes):
    return functools.reduce(lax.psum, axes, value)


def with_above(field, plane, axis):
    rest = lax.slice_in_dim(field, 1, field.shape[axis], axis=axis)
    return jnp.concatenate([rest, jnp.expand_dims(plane, axis)], axis)


def with_below(field, plane, axis):
    rest = lax.slice_in_dim(field, 0, field.shape[axis] - 1, axis=axis)
    return jnp.concatenate([jnp.expand_dims(plane, axis), rest], axis)


def above_joint(planes_x, planes_y, planes_z):
    return (
        passed_along(planes_x, GX, -1),
        passed_along(planes_y, GY, -1),
        passed_along(planes_z, "gz", -1),
    )


def below_joint(planes_x, planes_y, planes_z):
    return (
        passed_along(planes_x, GX, 1),
        passed_along(planes_y, GY, 1),
        passed_along(planes_z, "gz", 1),
    )


def advance(states, keep, curl, fetch_above, fetch_below):
    planes_x = jnp.stack(
        [plane for electric, magnetic in states for plane in (electric[1][0], electric[2][0])]
    )
    planes_y = jnp.stack(
        [plane for electric, magnetic in states for plane in (electric[0][:, 0], electric[2][:, 0])]
    )
    planes_z = jnp.stack(
        [
            plane
            for electric, magnetic in states
            for plane in (electric[0][:, :, 0], electric[1][:, :, 0])
        ]
    )
    above_x, above_y, above_z = fetch_above(planes_x, planes_y, planes_z)
    halfway = []
    for place, (electric, magnetic) in enumerate(states):
        electric_x, electric_y, electric_z = electric
        magnetic_x, magnetic_y, magnetic_z = magnetic
        magnetic_x = magnetic_x - 0.5 * (
            with_above(electric_z, above_y[2 * place + 1], 1)
            - electric_z
            - (with_above(electric_y, above_z[2 * place + 1], 2) - electric_y)
        )
        magnetic_y = magnetic_y - 0.5 * (
            with_above(electric_x, above_z[2 * place], 2)
            - electric_x
            - (with_above(electric_z, above_x[2 * place + 1], 0) - electric_z)
        )
        magnetic_z = magnetic_z - 0.5 * (
            with_above(electric_y, above_x[2 * place], 0)
            - electric_y
            - (with_above(electric_x, above_y[2 * place], 1) - electric_x)
        )
        halfway.append((electric, (magnetic_x, magnetic_y, magnetic_z)))
    planes_x = jnp.stack(
        [plane for electric, magnetic in halfway for plane in (magnetic[1][-1], magnetic[2][-1])]
    )
    planes_y = jnp.stack(
        [
            plane
            for electric, magnetic in halfway
            for plane in (magnetic[0][:, -1], magnetic[2][:, -1])
        ]
    )
    planes_z = jnp.stack(
        [
            plane
            for electric, magnetic in halfway
            for plane in (magnetic[0][:, :, -1], magnetic[1][:, :, -1])
        ]
    )
    below_x, below_y, below_z = fetch_below(planes_x, planes_y, planes_z)
    result = []
    for place, (electric, magnetic) in enumerate(halfway):
        electric_x, electric_y, electric_z = electric
        magnetic_x, magnetic_y, magnetic_z = magnetic
        electric_x = keep * electric_x + curl * (
            magnetic_z
            - with_below(magnetic_z, below_y[2 * place + 1], 1)
            - (magnetic_y - with_below(magnetic_y, below_z[2 * place + 1], 2))
        )
        electric_y = keep * electric_y + curl * (
            magnetic_x
            - with_below(magnetic_x, below_z[2 * place], 2)
            - (magnetic_z - with_below(magnetic_z, below_x[2 * place + 1], 0))
        )
        electric_z = keep * electric_z + curl * (
            magnetic_y
            - with_below(magnetic_y, below_x[2 * place], 0)
            - (magnetic_x - with_below(magnetic_x, below_y[2 * place], 1))
        )
        result.append(((electric_x, electric_y, electric_z), magnetic))
    return result


def locate(flat, shape, totals, offsets):
    first = flat // (totals[1] * totals[2]) - offsets[0]
    second = flat // totals[2] % totals[1] - offsets[1]
    third = flat % totals[2] - offsets[2]
    inside = (
        (first >= 0)
        & (first < shape[0])
        & (second >= 0)
        & (second < shape[1])
        & (third >= 0)
        & (third < shape[2])
    )
    first = jnp.clip(first, 0, shape[0] - 1)
    second = jnp.clip(second, 0, shape[1] - 1)
    third = jnp.clip(third, 0, shape[2] - 1)
    return (first, second, third, inside)


def inject(electric, spot, values):
    first, second, third, inside = spot
    added = electric[2].at[first, second, third].add(jnp.where(inside, values, 0.0))
    return (electric[0], electric[1], added)


def correlate(snapshots, adjoints, shape):
    gradient = jnp.zeros(shape, jnp.float32)
    for index in range(STEPS):
        later = STEPS - index
        adjoint = adjoints[index]
        change = [snapshots[later][c] - snapshots[later - 1][c] for c in range(3)]
        gradient = gradient + (
            change[0] * adjoint[0] + change[1] * adjoint[1] + change[2] * adjoint[2]
        )
    return gradient


def per_device(
    permittivity,
    loss,
    fwd_electric,
    fwd_magnetic,
    adj_electric,
    adj_magnetic,
    wavelet,
    residuals,
    source_cell,
    receiver_cells,
    start_step,
):
    shape = permittivity.shape
    totals = (
        shape[0] * lax.axis_size(GX),
        shape[1] * lax.axis_size(GY),
        shape[2] * lax.axis_size("gz"),
    )
    offsets = (
        lax.axis_index(GX) * shape[0],
        lax.axis_index(GY) * shape[1],
        lax.axis_index("gz") * shape[2],
    )
    keep = (1.0 - loss) / (1.0 + loss)
    curl = 0.5 / (permittivity * (1.0 + loss))
    start = start_step[0]
    window = lax.dynamic_slice_in_dim(residuals, start, STEPS, 1)
    samples = gather_all_axes(window, GX_GY_GZ, 0)
    forward = (
        (fwd_electric[0], fwd_electric[1], fwd_electric[2]),
        (fwd_magnetic[0], fwd_magnetic[1], fwd_magnetic[2]),
    )
    backward = (
        (adj_electric[0], adj_electric[1], adj_electric[2]),
        (adj_magnetic[0], adj_magnetic[1], adj_magnetic[2]),
    )
    snapshots = [forward[0]]
    adjoints = []
    source_spot = locate(source_cell[0], shape, totals, offsets)
    receiver_spot = locate(receiver_cells, shape, totals, offsets)
    for index in range(STEPS):
        forward, backward = advance([forward, backward], keep, curl, above_joint, below_joint)
        pulse = lax.dynamic_slice_in_dim(wavelet, start + index, 1)[0]
        forward = (inject(forward[0], source_spot, pulse), forward[1])
        backward = (inject(backward[0], receiver_spot, samples[:, STEPS - 1 - index]), backward[1])
        snapshots.append(forward[0])
        adjoints.append(backward[0])
    gradient = -correlate(snapshots, adjoints, shape) / permittivity
    total = by_axis(jnp.sum(gradient * gradient), GX_GY_GZ)
    grad_rms = jnp.sqrt(total / (totals[0] * totals[1] * totals[2]) + 1e-06)
    return (gradient / grad_rms, grad_rms)


def solution(mesh):
    torus = Mesh(
        mesh.devices.reshape(4, 2, 2, 8, mesh.shape["gz"]), ("gx_0", "gx_1", "gy_0", "gy_1", "gz")
    )
    return jax.shard_map(
        per_device,
        mesh=torus,
        in_specs=(
            P(GX, GY, "gz"),
            P(GX, GY, "gz"),
            P(None, GX, GY, "gz"),
            P(None, GX, GY, "gz"),
            P(None, GX, GY, "gz"),
            P(None, GX, GY, "gz"),
            P(),
            P(GX_GY_GZ, None),
            P(),
            P(),
            P(),
        ),
        out_specs=(P(GX, GY, "gz"), P()),
        check_vma=False,
    )
```

profile of v0, /device:TPU:1, one launch (start us, length us, event | category | flops | bytes accessed | tf_op | source)
XLA Modules:
  0.0 526.8 jit_solution(7867263505441312143)
XLA Ops:
  5.8 5.1 collective-permute-start
  12.3 1.4 collective-permute-start.1
  21.1 6.0 %all-gather.25 = f32[2,1,4]{2,1,0:T(1,128)S(1)} all-gather(f32[1,1,4]{2,1,0:T(1,128)S(1)} %get-tuple-element.271), channel_id=2, replica_groups=mesh['gx_0'=4,'gx_1'=2,'gy_0'=2,'gy_1'=8,'gz'=2] {'gz'}, dimensions={0}, use_global_device_ids=true | all-gather | bytes 48 | tf_op jit(solution)/shard_map/all_gather | solution.py:29
  27.1 15.2 %all-gather.26 = f32[8,2,4]{2,1,0:T(2,128)S(1)} all-gather(f32[1,2,4]{2,1,0:T(2,128)S(1)} %bitcast.638), channel_id=3, replica_groups=mesh['gx_0'=4,'gx_1'=2,'gy_0'=2,'gy_1'=8,'gz'=2] {'gy_1'}, dimensions={0}, use_global_device_ids=true | all-gather | bytes 288 | tf_op jit(solution)/shard_map/all_gather | solution.py:29
  42.3 3.8 all-gather.2
  46.1 6.2 %all-gather.3 = f32[4,8,2,1,4]{1,4,3,2,0:T(4,128)S(1)} all-gather(f32[2,8,2,1,4]{1,4,3,2,0:T(4,128)S(1)} %copy.5711), channel_id=5, replica_groups=mesh['gx_0'=4,'gx_1'=2,'gy_0'=2,'gy_1'=8,'gz'=2] {'gx_1'}, dimensions={0}, use_global_device_ids=true | all-gather | bytes 1536 | tf_op jit(solution)/shard_map/all_gather | solution.py:29
  52.4 10.1 %all-gather.4 = f32[8,2,8,2,1,4]{2,5,4,3,1,0:T(4,128)S(1)} all-gather(f32[2,2,8,2,1,4]{2,5,4,3,1,0:T(4,128)S(1)} %bitcast.588), channel_id=6, replica_groups=mesh['gx_0'=4,'gx_1'=2,'gy_0'=2,'gy_1'=8,'gz'=2] {'gx_0'}, dimensions={0}, use_global_device_ids=true | all-gather | bytes 5120 | tf_op jit(solution)/shard_map/all_gather | solution.py:29
  62.8 9.8 %all-gather.27 = f32[8,2,4]{2,1,0:T(2,128)S(1)} all-gather(f32[1,2,4]{2,1,0:T(2,128)S(1)} %get-tuple-element.269), channel_id=7, replica_groups=mesh['gx_0'=4,'gx_1'=2,'gy_0'=2,'gy_1'=8,'gz'=2] {'gy_1'}, dimensions={0}, use_global_device_ids=true | all-gather | bytes 288 | tf_op jit(solution)/shard_map/all_gather | solution.py:29
  72.6 3.6 all-gather.6
  76.3 9.0 %all-gather.7 = f32[4,8,2,4]{1,3,2,0:T(4,128)S(1)} all-gather(f32[2,8,2,4]{1,3,2,0:T(4,128)S(1)} %copy.5715), channel_id=9, replica_groups=mesh['gx_0'=4,'gx_1'=2,'gy_0'=2,'gy_1'=8,'gz'=2] {'gx_1'}, dimensions={0}, use_global_device_ids=true | all-gather | bytes 1536 | tf_op jit(solution)/shard_map/all_gather | solution.py:29
  85.2 9.0 %all-gather.8 = f32[8,2,8,2,4]{2,4,3,1,0:T(4,128)S(1)} all-gather(f32[2,2,8,2,4]{2,4,3,1,0:T(4,128)S(1)} %bitcast.589), channel_id=10, replica_groups=mesh['gx_0'=4,'gx_1'=2,'gy_0'=2,'gy_1'=8,'gz'=2] {'gx_0'}, dimensions={0}, use_global_device_ids=true | all-gather | bytes 5120 | tf_op jit(solution)/shard_map/all_gather | solution.py:29
  94.2 6.2 %all-gather.9 = f32[8,2,2,8,2,4]{3,1,0,5,4,2:T(2,128)S(1)} all-gather(f32[4,2,2,8,2,4]{3,1,0,5,4,2:T(2,128)S(1)} %bitcast.576), channel_id=11, replica_groups=mesh['gx_0'=4,'gx_1'=2,'gy_0'=2,'gy_1'=8,'gz'=2] {'gz'}, dimensions={0}, use_global_device_ids=true | all-gather | bytes 12288 | tf_op jit(solution)/shard_map/all_gather | solution.py:29
  100.9 3.2 all-gather.28
  104.1 6.5 %all-gather.29 = f32[2,2,4]{2,1,0:T(2,128)S(1)} all-gather(f32[1,2,4]{2,1,0:T(2,128)S(1)} %bitcast.639), channel_id=13, replica_groups=mesh['gx_0'=4,'gx_1'=2,'gy_0'=2,'gy_1'=8,'gz'=2] {'gx_1'}, dimensions={0}, use_global_device_ids=true | all-gather | bytes 96 | tf_op jit(solution)/shard_map/all_gather | solution.py:29
  110.7 8.1 %all-gather.12 = f32[8,2,1,4]{3,1,2,0:T(2,128)S(1)} all-gather(f32[2,2,1,4]{3,1,2,0:T(2,128)S(1)} %bitcast.637), channel_id=14, replica_groups=mesh['gx_0'=4,'gx_1'=2,'gy_0'=2,'gy_1'=8,'gz'=2] {'gx_0'}, dimensions={0}, use_global_device_ids=true | all-gather | bytes 320 | tf_op jit(solution)/shard_map/all_gather | solution.py:29
  118.8 5.0 all-gather.13
  123.8 18.5 %all-gather.14 = f32[16,4,2,2,1,4]{5,1,4,3,2,0:T(4,128)S(1)} all-gather(f32[2,4,2,2,1,4]{5,1,4,3,2,0:T(4,128)S(1)} %copy.5722), channel_id=16, replica_groups=mesh['gx_0'=4,'gx_1'=2,'gy_0'=2,'gy_1'=8,'gz'=2] {'gy_1'}, dimensions={0}, use_global_device_ids=true | all-gather | bytes 4608 | tf_op jit(solution)/shard_map/all_gather | solution.py:29
  143.0 11.0 %all-gather.30 = f32[2,2,4]{2,1,0:T(2,128)S(1)} all-gather(f32[1,2,4]{2,1,0:T(2,128)S(1)} %get-tuple-element.268), channel_id=17, replica_groups=mesh['gx_0'=4,'gx_1'=2,'gy_0'=2,'gy_1'=8,'gz'=2] {'gx_1'}, dimensions={0}, use_global_device_ids=true | all-gather | bytes 96 | tf_op jit(solution)/shard_map/all_gather | solution.py:29
  154.0 8.1 %all-gather.16 = f32[8,2,4]{2,1,0:T(2,128)S(1)} all-gather(f32[2,2,4]{2,1,0:T(2,128)S(1)} %all-gather.30), channel_id=18, replica_groups=mesh['gx_0'=4,'gx_1'=2,'gy_0'=2,'gy_1'=8,'gz'=2] {'gx_0'}, dimensions={0}, use_global_device_ids=true | all-gather | bytes 320 | tf_op jit(solution)/shard_map/all_gather | solution.py:29
  162.2 5.0 all-gather.17
  167.2 18.2 %all-gather.18 = f32[16,4,2,2,4]{4,1,3,2,0:T(4,128)S(1)} all-gather(f32[2,4,2,2,4]{4,1,3,2,0:T(4,128)S(1)} %copy.5726), channel_id=20, replica_groups=mesh['gx_0'=4,'gx_1'=2,'gy_0'=2,'gy_1'=8,'gz'=2] {'gy_1'}, dimensions={0}, use_global_device_ids=true | all-gather | bytes 4608 | tf_op jit(solution)/shard_map/all_gather | solution.py:29
  185.4 4.5 all-gather.19
  190.0 6.7 %all-gather.31 = f32[4,2,4]{2,1,0:T(2,128)S(1)} all-gather(f32[1,2,4]{2,1,0:T(2,128)S(1)} %get-tuple-element.267), channel_id=22, replica_groups=mesh['gx_0'=4,'gx_1'=2,'gy_0'=2,'gy_1'=8,'gz'=2] {'gx_0'}, dimensions={0}, use_global_device_ids=true | all-gather | bytes 160 | tf_op jit(solution)/shard_map/all_gather | solution.py:29
  196.7 4.7 all-gather.21
  201.4 18.2 %all-gather.22 = f32[16,4,2,4]{3,1,2,0:T(4,128)S(1)} all-gather(f32[2,4,2,4]{3,1,2,0:T(4,128)S(1)} %copy.5729), channel_id=24, replica_groups=mesh['gx_0'=4,'gx_1'=2,'gy_0'=2,'gy_1'=8,'gz'=2] {'gy_1'}, dimensions={0}, use_global_device_ids=true | all-gather | bytes 2304 | tf_op jit(solution)/shard_map/all_gather | solution.py:29
  219.6 3.8 all-gather.23
  223.6 23.6 %all-gather.24 = f32[4,8,2,4,2,4]{1,5,4,3,2,0:T(4,128)S(1)} all-gather(f32[2,8,2,4,2,4]{1,5,4,3,2,0:T(4,128)S(1)} %copy.5730), channel_id=26, replica_groups=mesh['gx_0'=4,'gx_1'=2,'gy_0'=2,'gy_1'=8,'gz'=2] {'gx_1'}, dimensions={0}, use_global_device_ids=true | all-gather | bytes 12288 | tf_op jit(solution)/shard_map/all_gather | solution.py:29
  248.7 2.0 copy.5732
  265.2 1.6 fusion.17
  269.1 2.4 collective-permute-start.3
  272.0 5.2 collective-permute-start.4
  277.2 2.6 collective-permute-start.5
  287.2 12.1 %scatter_fusion = f32[32768]{0:T(1024)S(1)} fusion(f32[32768]{0:T(1024)S(1)} %bitcast.485, s32[2048]{0:T(1024)S(1)} %broadcast_select_fusion.4, f32[2048]{0:T(1024)S(1)} %copy-done.70), kind=kCustom, calls=%fused_computation | custom fusion | flops 2048 | bytes 32768
  301.6 1.3 collective-permute-start.8
  303.0 2.5 collective-permute-start.6
  305.5 1.3 collective-permute-start.7
  308.8 1.4 collective-permute-done.7
  313.3 3.4 collective-permute-start.9
  317.3 5.8 %collective-permute-start.10 = (f32[4,8,32]{2,1,0:T(8,128)S(1)}, f32[4,8,32]{2,1,0:T(8,128)S(1)}, u32[]{:S(2)}, u32[]{:S(2)}) collective-permute-start(f32[4,8,32]{2,1,0:T(8,128)S(1)} %pad_maximum_fusion.15), channel_id=1, source_target_pairs={{0,1},{2,3},{4,5},{6,7},{8,9},{10,11},{12,13},{14,15},{16,17},{18,... | collective-permute-start | bytes 12296 | tf_op jit(solution)/shard_map/ppermute | solution.py:18
  323.1 3.6 collective-permute-start.11
  338.0 11.9 %scatter_fusion.1 = f32[32768]{0:T(1024)S(1)} fusion(f32[32768]{0:T(1024)S(1)} %bitcast.490, s32[2048]{0:T(1024)S(1)} %broadcast_select_fusion.4, f32[2048]{0:T(1024)S(1)} %copy-done.69), kind=kCustom, calls=%fused_computation.1 | custom fusion | flops 2048 | bytes 32768
  353.5 1.4 collective-permute-start.14
  355.0 1.9 collective-permute-start.12
  364.1 1.5 fusion.80
  369.1 4.7 collective-permute-start.17
  374.3 4.0 collective-permute-start.16
  378.3 4.3 collective-permute-start.15
  384.1 1.7 fusion.174
  396.3 11.9 %scatter_fusion.2 = f32[32768]{0:T(1024)S(1)} fusion(f32[32768]{0:T(1024)S(1)} %bitcast.495, s32[2048]{0:T(1024)S(1)} %broadcast_select_fusion.4, f32[2048]{0:T(1024)S(1)} %copy-done.68), kind=kCustom, calls=%fused_computation.2 | custom fusion | flops 2048 | bytes 32768
  413.7 1.5 collective-permute-start.19
  421.0 2.4 collective-permute-start.18
  429.0 1.6 fusion.116
  438.5 4.1 collective-permute-start.23
  442.6 1.6 copy.5799
  446.8 3.8 collective-permute-start.22
  450.6 4.1 collective-permute-start.21
  458.5 1.7 fusion.172
  463.7 12.2 %scatter_fusion.3 = f32[32768]{0:T(1024)S(1)} fusion(f32[32768]{0:T(1024)S(1)} %bitcast.500, s32[2048]{0:T(1024)S(1)} %broadcast_select_fusion.4, f32[2048]{0:T(1024)} %get-tuple-element.98), kind=kCustom, calls=%fused_computation.3 | custom fusion | flops 2048 | bytes 32768
  476.6 4.0 multiply_reduce_fusion
  480.6 7.3 %psum.35 = f32[]{:T(128)} all-reduce(f32[]{:T(128)} %get-tuple-element.96), channel_id=1, replica_groups=mesh['gx_0'=4,'gx_1'=2,'gy_0'=2,'gy_1'=8,'gz'=2] {'gx_0'}, use_global_device_ids=true, to_apply=%region_6.7 | all-reduce | flops 1 | bytes 8 | tf_op jit(solution)/shard_map/psum | solution.py:55
  487.9 5.6 %psum.36 = f32[]{:T(128)} all-reduce(f32[]{:T(128)} %psum.35), channel_id=1, replica_groups=mesh['gx_0'=4,'gx_1'=2,'gy_0'=2,'gy_1'=8,'gz'=2] {'gx_1'}, use_global_device_ids=true, to_apply=%region_7.8 | all-reduce | flops 1 | bytes 8 | tf_op jit(solution)/shard_map/psum | solution.py:55
  493.5 11.1 %psum.37 = f32[]{:T(128)} all-reduce(f32[]{:T(128)} %psum.36), channel_id=1, replica_groups=mesh['gx_0'=4,'gx_1'=2,'gy_0'=2,'gy_1'=8,'gz'=2] {'gy_0'}, use_global_device_ids=true, to_apply=%region_8.9 | all-reduce | flops 1 | bytes 8 | tf_op jit(solution)/shard_map/psum | solution.py:55
  504.6 12.7 %psum.38 = f32[]{:T(128)} all-reduce(f32[]{:T(128)} %psum.37), channel_id=1, replica_groups=mesh['gx_0'=4,'gx_1'=2,'gy_0'=2,'gy_1'=8,'gz'=2] {'gy_1'}, use_global_device_ids=true, to_apply=%region_9.10 | all-reduce | flops 1 | bytes 8 | tf_op jit(solution)/shard_map/psum | solution.py:55
  517.3 5.9 %psum.39 = f32[]{:T(128)} all-reduce(f32[]{:T(128)} %psum.38), channel_id=1, replica_groups=mesh['gx_0'=4,'gx_1'=2,'gy_0'=2,'gy_1'=8,'gz'=2] {'gz'}, use_global_device_ids=true, to_apply=%region_10.11 | all-reduce | flops 1 | bytes 8 | tf_op jit(solution)/shard_map/psum | solution.py:55
  (536 shorter events, 112.4 us)
Async XLA Ops:
  0.6 15.8 %copy-start = (f32[8,64]{1,0:T(8,128)S(1)}, f32[8,64]{1,0:T(8,128)}, u32[]{:S(2)}) copy-start(f32[8,64]{1,0:T(8,128)} %param.26) | copy-start | bytes 6148
  2.7 277.8 %copy-start.7 = (f32[1,8,32,128]{3,2,1,0:T(8,128)}, f32[1,8,32,128]{3,2,1,0:T(8,128)S(1)}, u32[]{:S(2)}) copy-start(f32[1,8,32,128]{3,2,1,0:T(8,128)S(1)} %get-tuple-element.129) | copy-start | bytes 393220
  2.7 279.7 %copy-start.5 = (f32[1,8,32,128]{3,2,1,0:T(8,128)}, f32[1,8,32,128]{3,2,1,0:T(8,128)S(1)}, u32[]{:S(2)}) copy-start(f32[1,8,32,128]{3,2,1,0:T(8,128)S(1)} %get-tuple-element.127) | copy-start | bytes 393220
  2.8 279.7 %copy-start.6 = (f32[1,8,32,128]{3,2,1,0:T(8,128)}, f32[1,8,32,128]{3,2,1,0:T(8,128)S(1)}, u32[]{:S(2)}) copy-start(f32[1,8,32,128]{3,2,1,0:T(8,128)S(1)} %get-tuple-element.128) | copy-start | bytes 393220
  2.8 2.3 copy-start.15
  3.8 258.5 %collective-permute-start.2 = (f32[4,8,32]{2,1,0:T(8,128)}, f32[4,8,32]{2,1,0:T(8,128)}, u32[]{:S(2)}, u32[]{:S(2)}) collective-permute-start(f32[4,8,32]{2,1,0:T(8,128)} %pad_maximum_fusion.9), channel_id=1, source_target_pairs={{1,0},{3,2},{5,4},{7,6},{9,8},{11,10},{13,12},{15,14},{17,16},{19,... | collective-permute-start | bytes 12296 | tf_op jit(solution)/shard_map/ppermute | solution.py:18
  5.8 258.6 %collective-permute-start = (f32[4,32,128]{2,1,0:T(8,128)}, f32[4,32,128]{2,1,0:T(8,128)}, u32[]{:S(2)}, u32[]{:S(2)}) collective-permute-start(f32[4,32,128]{2,1,0:T(8,128)} %pad_maximum_fusion), channel_id=1, source_target_pairs={{32,0},{64,32},{96,64},{128,96},{160,128},{192,160},{224,192},{33,... | collective-permute-start | bytes 196616 | tf_op jit(solution)/shard_map/ppermute | solution.py:18
  11.6 2.8 copy-start.34
  12.3 4.3 copy-start.54
  12.3 251.4 %collective-permute-start.1 = (f32[4,8,128]{2,1,0:T(8,128)}, f32[4,8,128]{2,1,0:T(8,128)}, u32[]{:S(2)}, u32[]{:S(2)}) collective-permute-start(f32[4,8,128]{2,1,0:T(8,128)} %pad_maximum_fusion.8), channel_id=1, source_target_pairs={{2,0},{4,2},{6,4},{8,6},{10,8},{12,10},{14,12},{16,14},{18,16},{20... | collective-permute-start | bytes 49160 | tf_op jit(solution)/shard_map/ppermute | solution.py:18
  263.4 1.8 copy-start.31
  263.5 1.7 copy-start.29
  263.5 1.7 copy-start.30
  269.1 11.4 %collective-permute-start.3 = (f32[4,8,128]{2,1,0:T(8,128)S(1)}, f32[4,8,128]{2,1,0:T(8,128)S(1)}, u32[]{:S(2)}, u32[]{:S(2)}) collective-permute-start(f32[4,8,128]{2,1,0:T(8,128)S(1)} %pad_maximum_fusion.10), channel_id=1, source_target_pairs={{0,2},{2,4},{4,6},{6,8},{8,10},{10,12},{12,14},{14,16},{16,18},{18... | collective-permute-start | bytes 49160 | tf_op jit(solution)/shard_map/ppermute | solution.py:18
  272.0 7.9 %collective-permute-start.4 = (f32[4,8,32]{2,1,0:T(8,128)S(1)}, f32[4,8,32]{2,1,0:T(8,128)S(1)}, u32[]{:S(2)}, u32[]{:S(2)}) collective-permute-start(f32[4,8,32]{2,1,0:T(8,128)S(1)} %pad_maximum_fusion.11), channel_id=1, source_target_pairs={{0,1},{2,3},{4,5},{6,7},{8,9},{10,11},{12,13},{14,15},{16,17},{18,... | collective-permute-start | bytes 12296 | tf_op jit(solution)/shard_map/ppermute | solution.py:18
  277.2 5.1 collective-permute-start.5
  301.6 6.0 %collective-permute-start.8 = (f32[4,8,32]{2,1,0:T(8,128)S(1)}, f32[4,8,32]{2,1,0:T(8,128)S(1)}, u32[]{:S(2)}, u32[]{:S(2)}) collective-permute-start(f32[4,8,32]{2,1,0:T(8,128)S(1)} %pad_maximum_fusion.13), channel_id=1, source_target_pairs={{1,0},{3,2},{5,4},{7,6},{9,8},{11,10},{13,12},{15,14},{17,16},{19,... | collective-permute-start | bytes 12296 | tf_op jit(solution)/shard_map/ppermute | solution.py:18
  303.0 7.2 %collective-permute-start.6 = (f32[4,32,128]{2,0,1:T(4,128)S(1)}, f32[4,32,128]{2,0,1:T(4,128)S(1)}, u32[]{:S(2)}, u32[]{:S(2)}) collective-permute-start(f32[4,32,128]{2,0,1:T(4,128)S(1)} %pad_maximum_fusion.2), channel_id=1, source_target_pairs={{32,0},{64,32},{96,64},{128,96},{160,128},{192,160},{224,192},{33,... | collective-permute-start | bytes 196616 | tf_op jit(solution)/shard_map/ppermute | solution.py:18
  305.5 4.6 collective-permute-start.7
  310.2 1.9 copy-start.48
  313.3 14.0 %collective-permute-start.9 = (f32[4,8,128]{2,1,0:T(8,128)S(1)}, f32[4,8,128]{2,1,0:T(8,128)S(1)}, u32[]{:S(2)}, u32[]{:S(2)}) collective-permute-start(f32[4,8,128]{2,1,0:T(8,128)S(1)} %pad_maximum_fusion.14), channel_id=1, source_target_pairs={{0,2},{2,4},{4,6},{6,8},{8,10},{10,12},{12,14},{14,16},{16,18},{18... | collective-permute-start | bytes 49160 | tf_op jit(solution)/shard_map/ppermute | solution.py:18
  317.3 9.4 %collective-permute-start.10 = (f32[4,8,32]{2,1,0:T(8,128)S(1)}, f32[4,8,32]{2,1,0:T(8,128)S(1)}, u32[]{:S(2)}, u32[]{:S(2)}) collective-permute-start(f32[4,8,32]{2,1,0:T(8,128)S(1)} %pad_maximum_fusion.15), channel_id=1, source_target_pairs={{0,1},{2,3},{4,5},{6,7},{8,9},{10,11},{12,13},{14,15},{16,17},{18,... | collective-permute-start | bytes 12296 | tf_op jit(solution)/shard_map/ppermute | solution.py:18
  323.1 4.9 collective-permute-start.11
  353.5 6.6 %collective-permute-start.14 = (f32[4,8,32]{2,1,0:T(8,128)S(1)}, f32[4,8,32]{2,1,0:T(8,128)S(1)}, u32[]{:S(2)}, u32[]{:S(2)}) collective-permute-start(f32[4,8,32]{2,1,0:T(8,128)S(1)} %pad_maximum_fusion.17), channel_id=1, source_target_pairs={{1,0},{3,2},{5,4},{7,6},{9,8},{11,10},{13,12},{15,14},{17,16},{19,... | collective-permute-start | bytes 12296 | tf_op jit(solution)/shard_map/ppermute | solution.py:18
  354.9 2.0 copy-start.79
  354.9 2.0 copy-start.81
  355.0 8.2 %collective-permute-start.12 = (f32[4,32,128]{2,0,1:T(4,128)S(1)}, f32[4,32,128]{2,0,1:T(4,128)S(1)}, u32[]{:S(2)}, u32[]{:S(2)}) collective-permute-start(f32[4,32,128]{2,0,1:T(4,128)S(1)} %pad_maximum_fusion.4), channel_id=1, source_target_pairs={{32,0},{64,32},{96,64},{128,96},{160,128},{192,160},{224,192},{33,... | collective-permute-start | bytes 196616 | tf_op jit(solution)/shard_map/ppermute | solution.py:18
  357.0 6.2 %collective-permute-start.13 = (f32[4,8,128]{2,1,0:T(8,128)S(1)}, f32[4,8,128]{2,1,0:T(8,128)S(1)}, u32[]{:S(2)}, u32[]{:S(2)}) collective-permute-start(f32[4,8,128]{2,1,0:T(8,128)S(1)} %pad_maximum_fusion.16), channel_id=1, source_target_pairs={{2,0},{4,2},{6,4},{8,6},{10,8},{12,10},{14,12},{16,14},{18,16},{20... | collective-permute-start | bytes 49160 | tf_op jit(solution)/shard_map/ppermute | solution.py:18
  364.1 1.6 copy-start.23
  364.1 1.6 copy-start.45
  364.1 1.6 copy-start.46
  369.1 15.0 %collective-permute-start.17 = (f32[4,32,128]{2,0,1:T(4,128)}, f32[4,32,128]{2,0,1:T(4,128)}, u32[]{:S(2)}, u32[]{:S(2)}) collective-permute-start(f32[4,32,128]{2,0,1:T(4,128)} %pad_maximum_fusion.5), channel_id=1, source_target_pairs={{0,32},{32,64},{64,96},{96,128},{128,160},{160,192},{192,224},{1,3... | collective-permute-start | bytes 196616 | tf_op jit(solution)/shard_map/ppermute | solution.py:18
  374.3 8.3 %collective-permute-start.16 = (f32[4,8,32]{2,1,0:T(8,128)S(1)}, f32[4,8,32]{2,1,0:T(8,128)S(1)}, u32[]{:S(2)}, u32[]{:S(2)}) collective-permute-start(f32[4,8,32]{2,1,0:T(8,128)S(1)} %pad_maximum_fusion.19), channel_id=1, source_target_pairs={{0,1},{2,3},{4,5},{6,7},{8,9},{10,11},{12,13},{14,15},{16,17},{18,... | collective-permute-start | bytes 12296 | tf_op jit(solution)/shard_map/ppermute | solution.py:18
  378.3 5.1 collective-permute-start.15
  390.7 26.1 %copy-start.2 = (f32[8,32,128]{2,0,1:T(8,128)}, f32[8,32,128]{2,0,1:T(8,128)S(1)}, u32[]{:S(2)}) copy-start(f32[8,32,128]{2,0,1:T(8,128)S(1)} %get-tuple-element.136) | copy-start | bytes 393220
  413.7 14.3 %collective-permute-start.19 = (f32[4,8,128]{2,1,0:T(8,128)}, f32[4,8,128]{2,1,0:T(8,128)}, u32[]{:S(2)}, u32[]{:S(2)}) collective-permute-start(f32[4,8,128]{2,1,0:T(8,128)} %pad_maximum_fusion.20), channel_id=1, source_target_pairs={{2,0},{4,2},{6,4},{8,6},{10,8},{12,10},{14,12},{16,14},{18,16},{20... | collective-permute-start | bytes 49160 | tf_op jit(solution)/shard_map/ppermute | solution.py:18
  418.2 2.0 copy-start.64
  418.2 2.0 copy-start.65
  418.9 6.0 %collective-permute-start.20 = (f32[4,8,32]{2,1,0:T(8,128)S(1)}, f32[4,8,32]{2,1,0:T(8,128)S(1)}, u32[]{:S(2)}, u32[]{:S(2)}) collective-permute-start(f32[4,8,32]{2,1,0:T(8,128)S(1)} %pad_maximum_fusion.21), channel_id=1, source_target_pairs={{1,0},{3,2},{5,4},{7,6},{9,8},{11,10},{13,12},{15,14},{17,16},{19,... | collective-permute-start | bytes 12296 | tf_op jit(solution)/shard_map/ppermute | solution.py:18
  421.0 7.8 %collective-permute-start.18 = (f32[4,32,128]{2,0,1:T(4,128)S(1)}, f32[4,32,128]{2,0,1:T(4,128)S(1)}, u32[]{:S(2)}, u32[]{:S(2)}) collective-permute-start(f32[4,32,128]{2,0,1:T(4,128)S(1)} %pad_maximum_fusion.6), channel_id=1, source_target_pairs={{32,0},{64,32},{96,64},{128,96},{160,128},{192,160},{224,192},{33,... | collective-permute-start | bytes 196616 | tf_op jit(solution)/shard_map/ppermute | solution.py:18
  428.8 2.5 copy-start.66
  428.8 1.8 copy-start.56
  428.8 2.4 copy-start.58
  428.9 2.3 copy-start.3
  428.9 2.3 copy-start.11
  428.9 2.3 copy-start.13
  428.9 2.3 copy-start.18
  429.0 2.3 copy-start.19
  429.0 2.3 copy-start.20
  429.0 2.3 copy-start.24
  429.0 2.3 copy-start.25
  429.0 2.3 copy-start.43
  430.6 5.8 %copy-start.8 = (f32[8,32,128]{2,0,1:T(8,128)}, f32[8,32,128]{2,0,1:T(8,128)S(1)}, u32[]{:S(2)}) copy-start(f32[8,32,128]{2,0,1:T(8,128)S(1)} %get-tuple-element.145) | copy-start | bytes 393220
  431.6 5.5 %copy-start.9 = (f32[8,32,128]{2,0,1:T(8,128)}, f32[8,32,128]{2,0,1:T(8,128)S(1)}, u32[]{:S(2)}) copy-start(f32[8,32,128]{2,0,1:T(8,128)S(1)} %get-tuple-element.141) | copy-start | bytes 393220
  438.5 20.0 %collective-permute-start.23 = (f32[4,32,128]{2,0,1:T(4,128)}, f32[4,32,128]{2,0,1:T(4,128)}, u32[]{:S(2)}, u32[]{:S(2)}) collective-permute-start(f32[4,32,128]{2,0,1:T(4,128)} %pad_maximum_fusion.7), channel_id=1, source_target_pairs={{0,32},{32,64},{64,96},{96,128},{128,160},{160,192},{192,224},{1,3... | collective-permute-start | bytes 196616 | tf_op jit(solution)/shard_map/ppermute | solution.py:18
  446.8 3.8 copy-start.80
  446.8 3.8 copy-start.83
  446.8 3.8 copy-start.85
  446.8 3.8 copy-start.86
  446.8 8.0 %collective-permute-start.22 = (f32[4,8,32]{2,1,0:T(8,128)S(1)}, f32[4,8,32]{2,1,0:T(8,128)S(1)}, u32[]{:S(2)}, u32[]{:S(2)}) collective-permute-start(f32[4,8,32]{2,1,0:T(8,128)S(1)} %pad_maximum_fusion.23), channel_id=1, source_target_pairs={{0,1},{2,3},{4,5},{6,7},{8,9},{10,11},{12,13},{14,15},{16,17},{18,... | collective-permute-start | bytes 12296 | tf_op jit(solution)/shard_map/ppermute | solution.py:18
  450.6 7.3 %collective-permute-start.21 = (f32[4,8,128]{2,1,0:T(8,128)S(1)}, f32[4,8,128]{2,1,0:T(8,128)S(1)}, u32[]{:S(2)}, u32[]{:S(2)}) collective-permute-start(f32[4,8,128]{2,1,0:T(8,128)S(1)} %pad_maximum_fusion.22), channel_id=1, source_target_pairs={{0,2},{2,4},{4,6},{6,8},{8,10},{10,12},{12,14},{14,16},{16,18},{18... | collective-permute-start | bytes 49160 | tf_op jit(solution)/shard_map/ppermute | solution.py:18
  457.1 3.1 copy-start.40
  457.9 2.3 copy-start.41
  463.7 12.2 %copy-start.4 = (f32[8,32,128]{2,0,1:T(8,128)S(1)}, f32[8,32,128]{2,0,1:T(8,128)}, u32[]{:S(2)}) copy-start(f32[8,32,128]{2,0,1:T(8,128)} %copy-done.2) | copy-start | bytes 393220
  (52 other events, 46.8 us)
where the time goes:
time: 533 us; the launch traced here: 527 us
  blocking collectives  267 us (50%)
  local copies, waits for them, and re-layouts  98.5 us (18%)
  other arithmetic  71.6 us (13%)
  starting transfers between devices  70.7 us (13%)
  between operations  15.8 us (3%)
    all_gather x25, blocking collectives, all_blocks(): pieces = lax.all_gather(pieces, axes[k])  224 us
    ppermute x24, starting transfers between devices, passed_along(): return lax.ppermute(block, axis, route)  70.7 us
    unnamed x7, other arithmetic  48.9 us
    psum x5, blocking collectives, by_axis(): return functools.reduce(lax.psum, axes, value)  42.6 us
    slice x52, local copies, waits for them, and re-layouts, with_above(): rest = lax.slice_in_dim(field, 1, field.shape[axis], axis=axis)  21.3 us
    unnamed x195, local copies, waits for them, and re-layouts  18.2 us
  transfers between devices with their start and end apart: 24, of which 5 were waited for; matrix products, arithmetic and copies ran while one was open for 8% of the time, Pallas kernels for 0%

commit v1 on v0

v1 whole, which is shorter than its diff:
```python
import functools

import jax
import jax.numpy as jnp
from jax import lax
from jax.experimental import pallas as pl
from jax.experimental.pallas import tpu as pltpu
from jax.sharding import PartitionSpec as P

STEPS = 4
MESH = pl.DeviceIdType.MESH
F32 = jnp.float32
BF16 = jnp.bfloat16

HALO = 4
OWNX = HALO
OWNY = 16
TOP = 8
ROWS = 48
FIRST = 8
COMPS = 14


def kernel(
    dims,
    perm_hbm,
    loss_hbm,
    fe_hbm,
    fm_hbm,
    ae_hbm,
    am_hbm,
    res_ref,
    cells_ref,
    wave_ref,
    source_ref,
    start_ref,
    out_ref,
    rms_ref,
    field,
    medium,
    ysend,
    yrecv,
    corner,
    pack,
    packedge,
    packrecv,
    packedgerecv,
    slab,
    snaps,
    grad,
    hrow,
    hslab,
    smask,
    sslab,
    onehot,
    inj,
    injslab,
    gather1,
    gather2,
    red1,
    red2,
    load_sem,
    halo_send,
    halo_recv,
    group_send,
    group_recv,
):
    ngx, ngy, ngz, nx, ny, nz, nrec = dims
    gx, gy, gz = lax.axis_index("gx"), lax.axis_index("gy"), lax.axis_index("gz")
    i1 = lax.rem(gy, 8) * 2 + gz
    i2 = gx * 2 + gy // 8
    own = (slice(OWNX, OWNX + nx), slice(OWNY, OWNY + ny))

    loads = []
    for k, (src, dst) in enumerate(
        (
            (perm_hbm, medium.at[0]),
            (loss_hbm, medium.at[1]),
            (fe_hbm, field.at[2:5, own[0], own[1]]),
            (fm_hbm, field.at[5:8, own[0], own[1]]),
            (ae_hbm, field.at[8:11, own[0], own[1]]),
            (am_hbm, field.at[11:14, own[0], own[1]]),
        )
    ):
        copy = pltpu.make_async_copy(src, dst, load_sem.at[k])
        copy.start()
        loads.append(copy)

    def there(dx, dy):
        ok = []
        if dx:
            ok.append((gx + dx >= 0) & (gx + dx < ngx))
        if dy:
            ok.append((gy + dy >= 0) & (gy + dy < ngy))
        if not ok:
            return None
        return functools.reduce(jnp.logical_and, ok)

    def guarded(cond, fn):
        if cond is None:
            fn()
        else:
            pl.when(cond)(fn)

    def clear_planes(low):
        def body(c, _):
            field[c, low : low + HALO, OWNY : OWNY + ny, :] = jnp.zeros((HALO, ny, nz), F32)
            return 0

        lax.fori_loop(0, COMPS, body, 0)

    pl.when(gx == 0)(lambda: clear_planes(0))
    pl.when(gx == ngx - 1)(lambda: clear_planes(OWNX + nx))

    def clear(ref):
        ref[...] = jnp.zeros(ref.shape, F32)

    def clear_loop(ref):
        def body(c, _):
            ref[c] = jnp.zeros(ref.shape[1:], F32)
            return 0

        lax.fori_loop(0, ref.shape[0], body, 0)

    for ys, dy in ((0, -1), (1, 1)):
        missing_y = (gy + dy < 0) | (gy + dy >= ngy)
        pl.when(missing_y)(lambda ys=ys: clear_loop(yrecv.at[ys]))
        for xs, dx in ((0, -1), (1, 1)):
            missing = missing_y | (gx + dx < 0) | (gx + dx >= ngx)
            pl.when(missing)(lambda xs=xs, ys=ys: clear_loop(corner.at[xs, ys]))
        for q, dx in ((0, -1), (1, 0), (2, 1)):
            missing = missing_y | (gx + dx < 0) | (gx + dx >= ngx) if dx else missing_y
            for z in range(2):
                pl.when(missing)(lambda z=z, q=q, ys=ys: clear(packedgerecv.at[z, q, ys]))
    for q, dx in ((0, -1), (2, 1)):
        missing = (gx + dx < 0) | (gx + dx >= ngx)
        for z in range(2):
            pl.when(missing)(lambda z=z, q=q: clear_loop(packrecv.at[z, q]))

    barrier = pltpu.get_barrier_semaphore()
    for dx in (-1, 0, 1):
        for dy in (-1, 0, 1):
            for dz in (0, 1):
                if dx or dy or dz:
                    peer = {"gx": gx + dx, "gy": gy + dy, "gz": gz if dz == 0 else 1 - gz}
                    guarded(
                        there(dx, dy),
                        lambda peer=peer: pl.semaphore_signal(
                            barrier, inc=1, device_id=peer, device_id_type=MESH
                        ),
                    )

    def member1(k):
        return {"gx": gx, "gy": (gy // 8) * 8 + k // 2, "gz": lax.rem(k, 2)}

    def member2(k):
        return {"gx": k // 2, "gy": lax.rem(k, 2) * 8 + lax.rem(gy, 8), "gz": gz}

    groups = ((i1, member1), (i2, member2))
    for mine, member in groups:
        for step in range(1, 16):
            pl.semaphore_signal(
                barrier, inc=1, device_id=member(lax.rem(mine + step, 16)), device_id_type=MESH
            )

    start = start_ref[0]
    lane8 = lax.broadcasted_iota(jnp.int32, (8, 128), 1)
    sub8 = lax.broadcasted_iota(jnp.int32, (8, 128), 0)

    time = lax.broadcasted_iota(jnp.int32, res_ref.shape, 1)
    rows = []
    for m in range(STEPS):
        column = jnp.sum(jnp.where(time == start + m, res_ref[...], 0.0), axis=1, keepdims=True)
        spread = jnp.where(lane8 - i1 * 8 == sub8, jnp.broadcast_to(column, (8, 128)), 0.0)
        rows.append(jnp.sum(spread, axis=0, keepdims=True))
    gather1[i1] = jnp.concatenate(rows, axis=0)

    count_x = 3 - (gx == 0).astype(jnp.int32) - (gx == ngx - 1).astype(jnp.int32)
    count_y = 3 - (gy == 0).astype(jnp.int32) - (gy == ngy - 1).astype(jnp.int32)
    pl.semaphore_wait(barrier, count_x * count_y * 2 - 1 + 30)

    def group_copy(round_, which, ref, step):
        mine, member = groups[which]
        peer = lax.rem(mine + step, 16)
        return pltpu.make_async_remote_copy(
            src_ref=ref.at[mine],
            dst_ref=ref.at[mine],
            send_sem=group_send.at[round_, step - 1],
            recv_sem=group_recv.at[round_, mine],
            device_id=member(peer),
            device_id_type=MESH,
        )

    def group_arrival(round_, which, ref, step):
        mine, member = groups[which]
        peer = lax.rem(mine + step, 16)
        return pltpu.make_async_remote_copy(
            src_ref=ref.at[mine],
            dst_ref=ref.at[peer],
            send_sem=group_send.at[round_, step - 1],
            recv_sem=group_recv.at[round_, peer],
            device_id=member(peer),
            device_id_type=MESH,
        )

    def group_start(round_, which, ref):
        for step in range(1, 16):
            group_copy(round_, which, ref, step).start()

    def group_wait(round_, which, ref):
        for step in range(1, 16):
            group_arrival(round_, which, ref, step).wait_recv()

    def group_drain(round_, which, ref):
        for step in range(1, 16):
            group_copy(round_, which, ref, step).wait_send()

    group_start(0, 0, gather1)

    loads[0].wait()
    loads[1].wait()

    def coefficients(i, _):
        loss = medium[1, i]
        field[0, OWNX + i, OWNY : OWNY + ny, :] = (1.0 - loss) / (1.0 + loss)
        field[1, OWNX + i, OWNY : OWNY + ny, :] = 0.5 / (medium[0, i] * (1.0 + loss))
        return 0

    lax.fori_loop(0, nx, coefficients, 0)
    loads[2].wait()
    loads[3].wait()

    sends = []
    number = [0]

    def remote(src, dst, dx, dy, dz, back):
        k = number[0]
        number[0] += 1

        def make(landing):
            return pltpu.make_async_remote_copy(
                src_ref=src,
                dst_ref=landing,
                send_sem=halo_send.at[k],
                recv_sem=halo_recv.at[k],
                device_id={"gx": gx + dx, "gy": gy + dy, "gz": gz if dz == 0 else 1 - gz},
                device_id_type=MESH,
            )

        guarded(there(dx, dy), lambda: make(dst).start())
        sends.append((there(dx, dy), make(dst)))
        return lambda: guarded(there(-dx, -dy), lambda: make(back).wait_recv())

    def side(d):
        return 0 if d == 1 else 1

    def start_halos(c0, c1):
        waits = []
        for dx in (1, -1):
            source = slice(OWNX + nx - HALO, OWNX + nx) if dx == 1 else slice(OWNX, OWNX + HALO)
            target = slice(0, HALO) if dx == 1 else slice(OWNX + nx, OWNX + nx + HALO)
            landing = field.at[c0:c1, target, OWNY : OWNY + ny]
            waits.append(
                remote(field.at[c0:c1, source, OWNY : OWNY + ny], landing, dx, 0, 0, landing)
            )
            cond, copy = sends.pop()
            waits.append(lambda cond=cond, copy=copy: guarded(cond, copy.wait_send))
        for dy in (1, -1):
            edge = 1 if dy == 1 else 0
            landing = yrecv.at[side(dy), c0:c1]
            waits.append(remote(ysend.at[edge, c0:c1], landing, 0, dy, 0, landing))
            for dx in (1, -1):
                part = slice(nx - HALO, nx) if dx == 1 else slice(0, HALO)
                landing = corner.at[side(dx), side(dy), c0:c1]
                waits.append(remote(ysend.at[edge, c0:c1, part], landing, dx, dy, 0, landing))
        return waits

    def start_slabs():
        waits = []
        for dz in (0, 1):
            for dx in (0, 1, -1):
                for dy in (0, 1, -1):
                    if not (dx or dy or dz):
                        continue
                    z_there = gz
                    z_here = gz if dz == 0 else 1 - gz
                    if dy == 0:
                        waits.append(
                            remote(
                                pack,
                                packrecv.at[z_there, 1 - dx],
                                dx,
                                dy,
                                dz,
                                packrecv.at[z_here, 1 - dx],
                            )
                        )
                    else:
                        edge = 1 if dy == 1 else 0
                        waits.append(
                            remote(
                                packedge.at[edge],
                                packedgerecv.at[z_there, 1 - dx, side(dy)],
                                dx,
                                dy,
                                dz,
                                packedgerecv.at[z_here, 1 - dx, side(dy)],
                            )
                        )
        return waits

    def pack_edges(c0, c1):
        def body(c, _):
            ysend[0, c] = field[c, own[0], OWNY : OWNY + HALO, :]
            ysend[1, c] = field[c, own[0], OWNY + ny - HALO : OWNY + ny, :]
            return 0

        lax.fori_loop(c0, c1, body, 0)

    lane32 = lax.broadcasted_iota(jnp.int32, (ny, 128), 1)
    quad = lane32 // 4
    lift = 4 * (1 - gz)

    def pack_slab(group):
        packed = jnp.zeros((ny, 128), F32)
        for part in range(4):
            comp = group * 4 + part
            if comp >= COMPS:
                continue
            for i in range(nx):
                base = (part // 2) * 64 + i * 8 + (part % 2) * 4
                moved = pltpu.roll(field[comp, OWNX + i, own[1], :], base + lift, axis=1)
                packed = jnp.where(quad == base // 4, moved, packed)
        pack[group] = packed
        packrecv[gz, 1, group] = packed
        packedge[0, group] = packed[0:HALO]
        packedge[1, group] = packed[ny - HALO : ny]

    pack_edges(0, FIRST)
    first_waits = start_halos(0, FIRST)
    loads[4].wait()
    loads[5].wait()
    for group in range(4):
        pack_slab(group)
    slab_waits = start_slabs()
    pack_edges(FIRST, COMPS)
    second_waits = start_halos(FIRST, COMPS)

    row = lax.broadcasted_iota(jnp.int32, (ROWS, 128), 0) + TOP
    lane = lax.broadcasted_iota(jnp.int32, (ROWS, 128), 1)
    row_y = row - OWNY + gy * ny
    hrow[...] = jnp.where(row_y >= 0, 0.5, 0.0)
    slab_x = lane // 8 - OWNX + gx * nx
    hslab[...] = jnp.where((row_y >= 0) & (slab_x >= 0), 0.5, 0.0)
    source = source_ref[0]
    total_y, total_z = ngy * ny, ngz * nz
    src_x = source // (total_y * total_z)
    src_y = lax.rem(source // total_z, total_y)
    src_z = lax.rem(source, total_z)
    in_row = row_y == src_y
    smask[...] = jnp.where(in_row & (lane + gz * nz == src_z), 1.0, 0.0)
    slab_z = lax.rem(lane, 8) + nz - HALO
    sslab[...] = jnp.where(in_row & (slab_x == src_x) & (slab_z == src_z), 1.0, 0.0)
    src_plane = src_x - gx * nx + OWNX

    cells = cells_ref[...]
    rec_x = cells // (total_y * total_z) - gx * nx + OWNX
    rec_y = lax.rem(cells // total_z, total_y) - gy * ny + OWNY - TOP
    rec_z = lax.rem(cells, total_z)
    in_x = (rec_x >= 0) & (rec_x < nx + 2 * HALO)
    in_y = (rec_y >= 0) & (rec_y < ROWS)
    rec_row = jnp.where(in_x & in_y, rec_x * ROWS + rec_y, -1)
    rec_lane = rec_z - gz * nz
    planes = nx + 2 * HALO - 2

    def build(i, _):
        ids = lax.broadcasted_iota(jnp.int32, (ROWS, nrec), 0) + (i + 1) * ROWS
        onehot[pl.ds(pl.multiple_of(i * ROWS, 16), ROWS), :] = jnp.where(ids == rec_row, 1.0, 0.0).astype(BF16)
        return 0

    lax.fori_loop(0, planes, build, 0)

    group_wait(0, 0, gather1)
    row_of_samples = gather1[0]
    for k in range(1, 16):
        row_of_samples = row_of_samples + gather1[k]
    gather2[i2] = row_of_samples
    group_start(1, 1, gather2)

    lane_r = lax.broadcasted_iota(jnp.int32, (ROWS, nz), 1)

    def assemble(c0, c1):
        zeros = jnp.zeros((HALO, nz), F32)

        def body(c, _):
            for i in range(nx + 2 * HALO):
                for ys in range(2):
                    if i < OWNX:
                        piece = corner[0, ys, c, i]
                    elif i < OWNX + nx:
                        piece = yrecv[ys, c, i - OWNX]
                    else:
                        piece = corner[1, ys, c, i - OWNX - nx]
                    if ys == 0:
                        field[c, i, TOP:OWNY, :] = jnp.concatenate([zeros, piece], axis=0)
                    else:
                        field[c, i, OWNY + ny : OWNY + ny + 8, :] = jnp.concatenate([piece, zeros], axis=0)
            return 0

        lax.fori_loop(c0, c1, body, 0)

    lane_p = lax.broadcasted_iota(jnp.int32, (ROWS, 128), 1)

    def assemble_slab(c0, c1):
        zeros = jnp.zeros((HALO, 128), F32)
        for group in range(c0 // 4, (c1 + 3) // 4):
            centre, beside = [], []
            for z in range(2):
                full = []
                for q in range(3):
                    full.append(
                        jnp.concatenate(
                            [
                                zeros,
                                packedgerecv[z, q, 0, group],
                                packrecv[z, q, group],
                                packedgerecv[z, q, 1, group],
                                zeros,
                            ],
                            axis=0,
                        )
                    )
                centre.append(full[1])
                beside.append(jnp.where(lax.rem(lane_p, 64) >= 32, full[0], full[2]))
            for part in range(4):
                comp = group * 4 + part
                if comp >= c1:
                    continue
                base = (part // 2) * 64 + (part % 2) * 4
                inner = [pltpu.roll(centre[z], (32 + 4 * z - base) % 128, axis=1) for z in range(2)]
                outer = [pltpu.roll(beside[z], (96 + 4 * z - base) % 128, axis=1) for z in range(2)]
                deep = lax.rem(lane_p, 8) >= 4
                inside = (lane_p >= 32) & (lane_p < 96)
                slab[comp, TOP : TOP + ROWS, :] = jnp.where(
                    inside, jnp.where(deep, inner[1], inner[0]), jnp.where(deep, outer[1], outer[0])
                )

    up_keep = jnp.where(gz == 0, 1.0, 0.0)
    down_keep = jnp.where(gz == 0, 0.0, 1.0)
    body_rows = slice(TOP, TOP + ROWS)
    rows_up = slice(TOP + 1, TOP + 1 + ROWS)
    rows_down = slice(TOP - 1, TOP - 1 + ROWS)

    def magnetic_half(b, step):
        def body(i, _):
            factor = hrow[...] * jnp.where(gx * nx + i - OWNX >= 0, 1.0, 0.0)
            ex, ey, ez = field[b, i, body_rows], field[b + 1, i, body_rows], field[b + 2, i, body_rows]
            turn = lax.rem(2 * 128 - 1 - HALO - 8 * i, 128)

            def deeper(value, comp):
                edge = pltpu.roll(slab[comp, body_rows], turn, axis=1) * up_keep
                return jnp.where(lane_r == nz - 1, edge, pltpu.roll(value, nz - 1, axis=1))

            field[b + 3, i, body_rows] = field[b + 3, i, body_rows] - factor * (
                (field[b + 2, i, rows_up] - ez) - (deeper(ey, b + 1) - ey)
            )
            field[b + 4, i, body_rows] = field[b + 4, i, body_rows] - factor * (
                (deeper(ex, b) - ex) - (field[b + 2, i + 1, body_rows] - ez)
            )
            field[b + 5, i, body_rows] = field[b + 5, i, body_rows] - factor * (
                (field[b + 1, i + 1, body_rows] - ey) - (field[b, i, rows_up] - ex)
            )
            return 0

        lax.fori_loop(step - 1, nx + 2 * HALO - step, body, 0)
        factor = hslab[...]
        ex, ey, ez = slab[b, body_rows], slab[b + 1, body_rows], slab[b + 2, body_rows]

        def along_x(value):
            return pltpu.roll(value, 120, axis=1)

        def along_z(value):
            return pltpu.roll(value, 127, axis=1)

        slab[b + 3, body_rows] = slab[b + 3, body_rows] - factor * (
            (slab[b + 2, rows_up] - ez) - (along_z(ey) - ey)
        )
        slab[b + 4, body_rows] = slab[b + 4, body_rows] - factor * (
            (along_z(ex) - ex) - (along_x(ez) - ez)
        )
        slab[b + 5, body_rows] = slab[b + 5, body_rows] - factor * (
            (along_x(ey) - ey) - (slab[b, rows_up] - ex)
        )

    def electric_half(b, step, extra, extra_slab):
        def body(i, _):
            keep, curl = field[0, i, body_rows], field[1, i, body_rows]
            hx, hy, hz = field[b + 3, i, body_rows], field[b + 4, i, body_rows], field[b + 5, i, body_rows]
            turn = lax.rem(2 * 128 - (HALO - 1) - 8 * i, 128)

            def shallower(value, comp):
                edge = pltpu.roll(slab[comp, body_rows], turn, axis=1) * down_keep
                return jnp.where(lane_r == 0, edge, pltpu.roll(value, 1, axis=1))

            field[b, i, body_rows] = keep * field[b, i, body_rows] + curl * (
                (hz - field[b + 5, i, rows_down]) - (hy - shallower(hy, b + 4))
            )
            field[b + 1, i, body_rows] = keep * field[b + 1, i, body_rows] + curl * (
                (hx - shallower(hx, b + 3)) - (hz - field[b + 5, i - 1, body_rows])
            )
            field[b + 2, i, body_rows] = (
                keep * field[b + 2, i, body_rows]
                + curl * ((hy - field[b + 4, i - 1, body_rows]) - (hx - field[b + 3, i, rows_down]))
                + extra(i)
            )
            return 0

        lax.fori_loop(step, nx + 2 * HALO - step, body, 0)
        if step == STEPS:
            return
        keep, curl = slab[0, body_rows], slab[1, body_rows]
        hx, hy, hz = slab[b + 3, body_rows], slab[b + 4, body_rows], slab[b + 5, body_rows]

        def along_x(value):
            return pltpu.roll(value, 8, axis=1)

        def along_z(value):
            return pltpu.roll(value, 1, axis=1)

        slab[b, body_rows] = keep * slab[b, body_rows] + curl * (
            (hz - slab[b + 5, rows_down]) - (hy - along_z(hy))
        )
        slab[b + 1, body_rows] = keep * slab[b + 1, body_rows] + curl * (
            (hx - along_z(hx)) - (hz - along_x(hz))
        )
        slab[b + 2, body_rows] = (
            keep * slab[b + 2, body_rows]
            + curl * ((hy - along_x(hy)) - (hx - slab[b + 3, rows_down]))
            + extra_slab()
        )

    def snapshot(n):
        def body(i, _):
            for c in range(3):
                snaps[n, c, i] = field[2 + c, OWNX + i, own[1], :]
            return 0

        lax.fori_loop(0, nx, body, 0)

    for wait in first_waits:
        wait()
    for wait in slab_waits:
        wait()
    snapshot(0)
    assemble(0, FIRST)
    assemble_slab(0, FIRST)
    for step in range(1, STEPS + 1):
        pulse = wave_ref[start + step - 1]
        magnetic_half(2, step)
        electric_half(
            2,
            step,
            lambda i: smask[...] * jnp.where(i == src_plane, pulse, 0.0),
            lambda: sslab[...] * pulse,
        )
        snapshot(step)

    group_wait(1, 1, gather2)
    samples = [
        jnp.concatenate([gather2[k][m : m + 1] for k in range(16)], axis=1) for m in range(STEPS)
    ]

    def split(value):
        high = value.astype(BF16).astype(F32)
        return high, value - high

    contract = (((1,), (1,)), ((), ()))
    lanes_of = lax.broadcasted_iota(jnp.int32, (nz, nrec), 0)
    at_lane = lanes_of == rec_lane
    for m in range(STEPS):
        high, low = split(samples[STEPS - 1 - m])
        weights = jnp.concatenate(
            [jnp.where(at_lane, high, 0.0).astype(BF16), jnp.where(at_lane, low, 0.0).astype(BF16)],
            axis=0,
        )
        count = planes - 2 * m
        both = lax.dot_general(
            onehot[m * ROWS : (m + count) * ROWS, :], weights, contract, preferred_element_type=F32
        )
        inj[m, 1 + m : 1 + m + count] = (both[:, :nz] + both[:, nz:]).reshape(count, ROWS, nz)
    rec_near = rec_x * 8 + rec_z - (nz - HALO)
    in_slab = in_x & (rec_z >= nz - HALO) & (rec_z < nz + HALO)
    slab_weights = jnp.where(lanes_of == jnp.where(in_slab, rec_near, -1), 1.0, 0.0).astype(BF16)
    at_row = lax.broadcasted_iota(jnp.int32, (ROWS, nrec), 0) == rec_y
    pieces = []
    for m in range(STEPS - 1):
        for value in split(samples[STEPS - 1 - m]):
            pieces.append(jnp.where(at_row, value, 0.0).astype(BF16))
    both = lax.dot_general(
        jnp.concatenate(pieces, axis=0), slab_weights, contract, preferred_element_type=F32
    )
    for m in range(STEPS - 1):
        at = 2 * m * ROWS
        injslab[m] = both[at : at + ROWS] + both[at + ROWS : at + 2 * ROWS]

    for wait in second_waits:
        wait()
    assemble(FIRST, COMPS)
    assemble_slab(FIRST, COMPS)
    for step in range(1, STEPS + 1):
        magnetic_half(8, step)
        electric_half(
            8, step, lambda i, m=step - 1: inj[m, i], lambda m=step - 1: injslab[m]
        )
        later = STEPS + 1 - step

        def correlate(i, square, step=step, later=later):
            term = None
            for c in range(3):
                change = snaps[later, c, i] - snaps[later - 1, c, i]
                product = change * field[8 + c, OWNX + i, own[1], :]
                term = product if term is None else term + product
            value = term if step == 1 else grad[i] + term
            if step == STEPS:
                value = -value / medium[0, i]
                square = square + value * value
            grad[i] = value
            return square

        square = lax.fori_loop(0, nx, correlate, jnp.zeros((ny, nz), F32))

    red1[i1] = jnp.sum(square, axis=0, keepdims=True)
    group_start(2, 0, red1)
    group_wait(2, 0, red1)
    total = red1[0]
    for k in range(1, 16):
        total = total + red1[k]
    red2[i2] = total
    group_start(3, 1, red2)
    group_wait(3, 1, red2)
    total = red2[0]
    for k in range(1, 16):
        total = total + red2[k]
    total = jnp.sum(total, axis=1, keepdims=True)
    cells_in_all = ngx * nx * ngy * ny * ngz * nz
    rms = jnp.sqrt(total / cells_in_all + 1e-06)
    rms_ref[...] = rms
    wide = jnp.broadcast_to(rms, (ny, nz))

    def scale(i, _):
        out_ref[i] = grad[i] / wide
        return 0

    lax.fori_loop(0, nx, scale, 0)
    for cond, copy in sends:
        guarded(cond, copy.wait_send)
    group_drain(0, 0, gather1)
    group_drain(1, 1, gather2)
    group_drain(2, 0, red1)
    group_drain(3, 1, red2)


def solution(mesh):
    ngx, ngy, ngz = mesh.shape["gx"], mesh.shape["gy"], mesh.shape["gz"]

    def per_device(
        permittivity,
        loss,
        fwd_electric,
        fwd_magnetic,
        adj_electric,
        adj_magnetic,
        wavelet,
        residuals,
        source_cell,
        receiver_cells,
        start_step,
    ):
        nx, ny, nz = permittivity.shape
        nrec = receiver_cells.shape[0]
        planes = nx + 2 * HALO
        dims = (ngx, ngy, ngz, nx, ny, nz, nrec)
        hbm = pl.BlockSpec(memory_space=pl.ANY)
        vmem = pl.BlockSpec(memory_space=pltpu.VMEM)
        smem = pl.BlockSpec(memory_space=pltpu.SMEM)
        direction, rms = pl.pallas_call(
            functools.partial(kernel, dims),
            out_shape=(
                jax.ShapeDtypeStruct((nx, ny, nz), F32),
                jax.ShapeDtypeStruct((1, 1), F32),
            ),
            in_specs=[hbm] * 6 + [vmem] * 2 + [smem] * 3,
            out_specs=(vmem, vmem),
            scratch_shapes=[
                pltpu.VMEM((COMPS, planes, 64, nz), F32),
                pltpu.VMEM((2, nx, ny, nz), F32),
                pltpu.VMEM((2, COMPS, nx, HALO, nz), F32),
                pltpu.VMEM((2, COMPS, nx, HALO, nz), F32),
                pltpu.VMEM((2, 2, COMPS, HALO, HALO, nz), F32),
                pltpu.VMEM((4, ny, 128), F32),
                pltpu.VMEM((2, 4, HALO, 128), F32),
                pltpu.VMEM((2, 3, 4, ny, 128), F32),
                pltpu.VMEM((2, 3, 2, 4, HALO, 128), F32),
                pltpu.VMEM((COMPS, 64, 128), F32),
                pltpu.VMEM((STEPS + 1, 3, nx, ny, nz), F32),
                pltpu.VMEM((nx, ny, nz), F32),
                pltpu.VMEM((ROWS, 128), F32),
                pltpu.VMEM((ROWS, 128), F32),
                pltpu.VMEM((ROWS, 128), F32),
                pltpu.VMEM((ROWS, 128), F32),
                pltpu.VMEM(((planes - 2) * ROWS, nrec), BF16),
                pltpu.VMEM((STEPS, planes, ROWS, nz), F32),
                pltpu.VMEM((STEPS - 1, ROWS, 128), F32),
                pltpu.VMEM((16, STEPS, 128), F32),
                pltpu.VMEM((16, STEPS, 128), F32),
                pltpu.VMEM((16, 1, 128), F32),
                pltpu.VMEM((16, 1, 128), F32),
                pltpu.SemaphoreType.DMA((6,)),
                pltpu.SemaphoreType.DMA((33,)),
                pltpu.SemaphoreType.DMA((33,)),
                pltpu.SemaphoreType.DMA((4, 15)),
                pltpu.SemaphoreType.DMA((4, 16)),
            ],
            compiler_params=pltpu.CompilerParams(
                collective_id=0, has_side_effects=True, vmem_limit_bytes=60 * 1024 * 1024
            ),
            name="window",
        )(
            permittivity,
            loss,
            fwd_electric,
            fwd_magnetic,
            adj_electric,
            adj_magnetic,
            residuals,
            receiver_cells.reshape(1, nrec),
            wavelet,
            source_cell,
            start_step,
        )
        return direction, rms.reshape(())

    field_spec = P(None, "gx", "gy", "gz")
    block_spec = P("gx", "gy", "gz")
    return jax.shard_map(
        per_device,
        mesh=mesh,
        in_specs=(
            block_spec,
            block_spec,
            field_spec,
            field_spec,
            field_spec,
            field_spec,
            P(),
            P(("gx", "gy", "gz"), None),
            P(),
            P(),
            P(),
        ),
        out_specs=(block_spec, P()),
        check_vma=False,
    )
```

time: 533 us -> 70.7 us (0.13); the launches traced: 527 us -> 70.5 us
  blocking collectives: 267 us -> 0 us
  local copies, waits for them, and re-layouts: 98.5 us -> 1.57 us
  other arithmetic: 71.6 us -> 0 us
  starting transfers between devices: 70.7 us -> 0 us
  Pallas kernels: 0 us -> 65.2 us
  between operations: 15.8 us -> 3.74 us
    all_gather x25 -> x0, blocking collectives: 224 us -> none  [all_blocks(): pieces = lax.all_gather(pieces, axes[k])]
    ppermute x24 -> x0, starting transfers between devices: 70.7 us -> none  [passed_along(): return lax.ppermute(block, axis, route)]
    pallas_call x0 -> x1, Pallas kernels: none -> 65.2 us  [per_device(): pl.pallas_call(functools.partial(kernel, dims), out_shape=(jax.ShapeDtype...]
    slice x158 -> x0, local copies, waits for them, and re-layouts: 49.7 us -> none  [the longest x52 21.3 us: with_above(): rest = lax.slice_in_dim(field, 1, field.shape[axis], axis=axis)]
    unnamed x7 -> x0, other arithmetic: 48.9 us -> none
    psum x5 -> x0, blocking collectives: 42.6 us -> none  [by_axis(): return functools.reduce(lax.psum, axes, value)]
    another operation x82 -> x0, local copies, waits for them, and re-layouts: 24.1 us -> none  [the longest x24 10.2 us: with_above(): return jnp.concatenate([rest, jnp.expand_dims(plane, axis)], axis)]
    unnamed x195 -> x1, local copies, waits for them, and re-layouts: 18.2 us -> 1.57 us
  transfers between devices with their start and end apart: 24 -> 0, of which waited for: 5 -> 0; matrix products, arithmetic and copies ran while one was open for 8% -> 0% of each run, Pallas kernels for 0% -> 0%
where the time goes in v1:
time: 70.7 us; the launch traced here: 70.5 us
  Pallas kernels  65.2 us (92%)
  between operations  3.74 us (5%)
  local copies, waits for them, and re-layouts  1.57 us (2%)
    pallas_call x1, Pallas kernels, per_device(): pl.pallas_call(functools.partial(kernel, dims), out_shape=(jax.ShapeDtype...  65.2 us
    unnamed x1, local copies, waits for them, and re-layouts  1.57 us

profile of v1, /device:TPU:1, one launch (start us, length us, event | category | flops | bytes accessed | tf_op | source)
XLA Modules:
  0.0 70.5 jit_solution(5678114295585084793)
XLA Ops:
  1.9 65.2 %window.1 = (f32[8,32,128]{2,1,0:T(8,128)}, f32[1,1]{1,0:T(1,128)}) custom-call(f32[8,32,128]{2,1,0:T(8,128)} %perm_hbm.1, f32[8,32,128]{2,1,0:T(8,128)} %loss_hbm.1, f32[3,8,32,128]{3,2,1,0:T(8,128)} %fe_hbm.1, f32[3,8,32,128]{3,2,1,0:T(8,128)} %fm_hbm.1, f32[3,8,32,128]{3,2,1,0:T(8,128)} %ae_hbm.1, f32[3,8,32,128]{3,2,1,0:T(8,128)} %am_hbm.1, ...), custom_call_target="tpu_custom_call" | custom-call | tf_op jit(solution)/shard_map/window/pallas_call | solution.py:686
  67.2 1.6 %copy.17 = f32[8,32,128]{2,1,0:T(8,128)} copy(f32[8,32,128]{2,1,0:T(8,128)} %get-tuple-element.8) | data formatting | bytes 262144

commit v2 on v1

--- a/solution.py
+++ b/solution.py
@@ -19,6 +19,7 @@
 ROWS = 48
 FIRST = 8
 COMPS = 14
+GROUP = 16
 
 
 def kernel(
@@ -451,6 +452,19 @@
     rows_up = slice(TOP + 1, TOP + 1 + ROWS)
     rows_down = slice(TOP - 1, TOP - 1 + ROWS)
 
+    def over_planes(low, high, body):
+        count = (high - low) // GROUP
+
+        def several(k, _):
+            for j in range(GROUP):
+                body(low + k * GROUP + j, 0)
+            return 0
+
+        if count:
+            lax.fori_loop(0, count, several, 0)
+        for i in range(low + count * GROUP, high):
+            body(i, 0)
+
     def magnetic_half(b, step):
         def body(i, _):
             factor = hrow[...] * jnp.where(gx * nx + i - OWNX >= 0, 1.0, 0.0)
@@ -472,7 +486,7 @@
             )
             return 0
 
-        lax.fori_loop(step - 1, nx + 2 * HALO - step, body, 0)
+        over_planes(step - 1, nx + 2 * HALO - step, body)
         factor = hslab[...]
         ex, ey, ez = slab[b, body_rows], slab[b + 1, body_rows], slab[b + 2, body_rows]
 
@@ -515,7 +529,7 @@
             )
             return 0
 
-        lax.fori_loop(step, nx + 2 * HALO - step, body, 0)
+        over_planes(step, nx + 2 * HALO - step, body)
         if step == STEPS:
             return
         keep, curl = slab[0, body_rows], slab[1, body_rows]

time: 70.7 us -> 56.6 us (0.80)
  Pallas kernels: 65.2 us -> 51.1 us
    pallas_call x1, Pallas kernels: 65.2 us -> 51.1 us  [per_device(): pl.pallas_call(functools.partial(kernel, dims), out_shape=(jax.ShapeDtype...]
where the time goes in v2:
time: 56.6 us; the launch traced here: 56.4 us
  Pallas kernels  51.1 us (90%)
  between operations  3.74 us (7%)
  local copies, waits for them, and re-layouts  1.57 us (3%)
    pallas_call x1, Pallas kernels, per_device(): pl.pallas_call(functools.partial(kernel, dims), out_shape=(jax.ShapeDtype...  51.1 us
    unnamed x1, local copies, waits for them, and re-layouts  1.57 us

profile of v2, /device:TPU:1, one launch (start us, length us, event | category | flops | bytes accessed | tf_op | source)
XLA Modules:
  0.0 56.4 jit_solution(17019605990620620253)
XLA Ops:
  1.9 51.1 %window.1 = (f32[8,32,128]{2,1,0:T(8,128)}, f32[1,1]{1,0:T(1,128)}) custom-call(f32[8,32,128]{2,1,0:T(8,128)} %perm_hbm.1, f32[8,32,128]{2,1,0:T(8,128)} %loss_hbm.1, f32[3,8,32,128]{3,2,1,0:T(8,128)} %fe_hbm.1, f32[3,8,32,128]{3,2,1,0:T(8,128)} %fm_hbm.1, f32[3,8,32,128]{3,2,1,0:T(8,128)} %ae_hbm.1, f32[3,8,32,128]{3,2,1,0:T(8,128)} %am_hbm.1, ...), custom_call_target="tpu_custom_call" | custom-call | tf_op jit(solution)/shard_map/window/pallas_call | solution.py:700
  53.1 1.6 %copy.17 = f32[8,32,128]{2,1,0:T(8,128)} copy(f32[8,32,128]{2,1,0:T(8,128)} %get-tuple-element.8) | data formatting | bytes 262144

commit v3 on v1

v3 whole, which is shorter than its diff:
```python
import functools

import jax
import jax.numpy as jnp
from jax import lax
from jax.experimental import pallas as pl
from jax.experimental.pallas import tpu as pltpu
from jax.sharding import PartitionSpec as P

STEPS = 4
MESH = pl.DeviceIdType.MESH
F32 = jnp.float32
BF16 = jnp.bfloat16

HALO = 4
OWNX = HALO
OWNY = 16
TOP = 8
ROWS = 48
KEEP, CURL = 6, 7
FIRST = 8
COMPS = 14


def kernel(
    dims,
    perm_hbm,
    loss_hbm,
    fe_hbm,
    fm_hbm,
    ae_hbm,
    am_hbm,
    res_hbm,
    cells_hbm,
    wave_hbm,
    source_hbm,
    start_hbm,
    out_ref,
    rms_ref,
    field,
    medium,
    ysend,
    yrecv,
    corner,
    res_ref,
    cells_ref,
    wave_ref,
    source_ref,
    start_ref,
    pack,
    packedge,
    packx,
    packxedge,
    packrecv,
    packedgerecv,
    packxrecv,
    packxedgerecv,
    slab,
    snaps,
    change,
    hrow,
    hslab,
    smask,
    sslab,
    onehot,
    inj,
    injslab,
    gather1,
    gather2,
    red1,
    red2,
    load_sem,
    halo_send,
    halo_recv,
    group_send,
    group_recv,
):
    ngx, ngy, ngz, nx, ny, nz, nrec = dims
    gx, gy, gz = lax.axis_index("gx"), lax.axis_index("gy"), lax.axis_index("gz")
    i1 = lax.rem(gy, 8) * 2 + gz
    i2 = gx * 2 + gy // 8
    own = (slice(OWNX, OWNX + nx), slice(OWNY, OWNY + ny))

    loads = {}
    for k, (name, src, dst) in enumerate(
        (
            ("fe", fe_hbm, field.at[0:3, own[0], own[1]]),
            ("fm", fm_hbm, field.at[3:6, own[0], own[1]]),
            ("perm", perm_hbm, medium.at[0]),
            ("loss", loss_hbm, medium.at[1]),
            ("start", start_hbm, start_ref),
            ("res", res_hbm, res_ref),
            ("ae", ae_hbm, field.at[8:11, own[0], own[1]]),
            ("am", am_hbm, field.at[11:14, own[0], own[1]]),
            ("source", source_hbm, source_ref),
            ("wave", wave_hbm, wave_ref),
            ("cells", cells_hbm, cells_ref),
        )
    ):
        loads[name] = pltpu.make_async_copy(src, dst, load_sem.at[k])
        loads[name].start()

    def there(dx, dy):
        ok = []
        if dx:
            ok.append((gx + dx >= 0) & (gx + dx < ngx))
        if dy:
            ok.append((gy + dy >= 0) & (gy + dy < ngy))
        if not ok:
            return None
        return functools.reduce(jnp.logical_and, ok)

    def guarded(cond, fn):
        if cond is None:
            fn()
        else:
            pl.when(cond)(fn)

    def clear_planes(low):
        def body(c, _):
            field[c, low : low + HALO, OWNY : OWNY + ny, :] = jnp.zeros((HALO, ny, nz), F32)
            return 0

        lax.fori_loop(0, COMPS, body, 0)

    pl.when(gx == 0)(lambda: clear_planes(0))
    pl.when(gx == ngx - 1)(lambda: clear_planes(OWNX + nx))

    def clear(ref):
        ref[...] = jnp.zeros(ref.shape, F32)

    def clear_loop(ref):
        def body(c, _):
            ref[c] = jnp.zeros(ref.shape[1:], F32)
            return 0

        lax.fori_loop(0, ref.shape[0], body, 0)

    for ys, dy in ((0, -1), (1, 1)):
        missing_y = (gy + dy < 0) | (gy + dy >= ngy)
        pl.when(missing_y)(lambda ys=ys: clear_loop(yrecv.at[ys]))
        for xs, dx in ((0, -1), (1, 1)):
            missing = missing_y | (gx + dx < 0) | (gx + dx >= ngx)
            pl.when(missing)(lambda xs=xs, ys=ys: clear_loop(corner.at[xs, ys]))
        for z in range(2):
            pl.when(missing_y)(lambda z=z, ys=ys: clear(packedgerecv.at[z, ys]))
            for xs, dx in ((0, -1), (1, 1)):
                missing = missing_y | (gx + dx < 0) | (gx + dx >= ngx)
                pl.when(missing)(lambda z=z, xs=xs, ys=ys: clear(packxedgerecv.at[z, xs, ys]))
    for xs, dx in ((0, -1), (1, 1)):
        missing = (gx + dx < 0) | (gx + dx >= ngx)
        for z in range(2):
            pl.when(missing)(lambda z=z, xs=xs: clear(packxrecv.at[z, xs]))

    barrier = pltpu.get_barrier_semaphore()
    for dx in (-1, 0, 1):
        for dy in (-1, 0, 1):
            for dz in (0, 1):
                if dx or dy or dz:
                    peer = {"gx": gx + dx, "gy": gy + dy, "gz": gz if dz == 0 else 1 - gz}
                    guarded(
                        there(dx, dy),
                        lambda peer=peer: pl.semaphore_signal(
                            barrier, inc=1, device_id=peer, device_id_type=MESH
                        ),
                    )

    def member1(k):
        return {"gx": gx, "gy": (gy // 8) * 8 + k // 2, "gz": lax.rem(k, 2)}

    def member2(k):
        return {"gx": k // 2, "gy": lax.rem(k, 2) * 8 + lax.rem(gy, 8), "gz": gz}

    groups = ((i1, member1), (i2, member2))
    for mine, member in groups:
        for step in range(1, 16):
            pl.semaphore_signal(
                barrier, inc=1, device_id=member(lax.rem(mine + step, 16)), device_id_type=MESH
            )

    loads["start"].wait()
    loads["res"].wait()
    start = start_ref[0]
    lane8 = lax.broadcasted_iota(jnp.int32, (8, 128), 1)
    sub8 = lax.broadcasted_iota(jnp.int32, (8, 128), 0)

    time = lax.broadcasted_iota(jnp.int32, res_ref.shape, 1)
    rows = []
    for m in range(STEPS):
        column = jnp.sum(jnp.where(time == start + m, res_ref[...], 0.0), axis=1, keepdims=True)
        spread = jnp.where(lane8 - i1 * 8 == sub8, jnp.broadcast_to(column, (8, 128)), 0.0)
        rows.append(jnp.sum(spread, axis=0, keepdims=True))
    gather1[i1] = jnp.concatenate(rows, axis=0)

    def group_copy(round_, which, ref, step):
        mine, member = groups[which]
        peer = lax.rem(mine + step, 16)
        return pltpu.make_async_remote_copy(
            src_ref=ref.at[mine],
            dst_ref=ref.at[mine],
            send_sem=group_send.at[round_, step - 1],
            recv_sem=group_recv.at[round_, mine],
            device_id=member(peer),
            device_id_type=MESH,
        )

    def group_arrival(round_, which, ref, step):
        mine, member = groups[which]
        peer = lax.rem(mine + step, 16)
        return pltpu.make_async_remote_copy(
            src_ref=ref.at[mine],
            dst_ref=ref.at[peer],
            send_sem=group_send.at[round_, step - 1],
            recv_sem=group_recv.at[round_, peer],
            device_id=member(peer),
            device_id_type=MESH,
        )

    def group_start(round_, which, ref):
        for step in range(1, 16):
            group_copy(round_, which, ref, step).start()

    def group_wait(round_, which, ref):
        for step in range(1, 16):
            group_arrival(round_, which, ref, step).wait_recv()

    def group_drain(round_, which, ref):
        for step in range(1, 16):
            group_copy(round_, which, ref, step).wait_send()

    sends = []
    number = [0]

    def remote(src, dst, dx, dy, dz, back):
        k = number[0]
        number[0] += 1

        def make(landing):
            return pltpu.make_async_remote_copy(
                src_ref=src,
                dst_ref=landing,
                send_sem=halo_send.at[k],
                recv_sem=halo_recv.at[k],
                device_id={"gx": gx + dx, "gy": gy + dy, "gz": gz if dz == 0 else 1 - gz},
                device_id_type=MESH,
            )

        guarded(there(dx, dy), lambda: make(dst).start())
        sends.append((there(dx, dy), make(dst)))
        return lambda: guarded(there(-dx, -dy), lambda: make(back).wait_recv())

    def side(d):
        return 0 if d == 1 else 1

    def span(low, count):
        return slice(low, low + count)

    def start_halos(c0, c1, low_parts, high_parts):
        waits, leaving = [], []
        rows_ = slice(OWNY, OWNY + ny)
        for dx, parts in ((1, low_parts), (-1, high_parts)):
            for first, last, depth in parts:
                if dx == 1:
                    source, target = span(OWNX + nx - depth, depth), span(HALO - depth, depth)
                else:
                    source, target = span(OWNX, depth), span(OWNX + nx, depth)
                landing = field.at[first:last, target, rows_]
                waits.append(remote(field.at[first:last, source, rows_], landing, dx, 0, 0, landing))
                cond, copy = sends.pop()
                leaving.append(lambda cond=cond, copy=copy: guarded(cond, copy.wait_send))
        for dy in (1, -1):
            edge = 1 if dy == 1 else 0
            landing = yrecv.at[side(dy), c0:c1]
            waits.append(remote(ysend.at[edge, c0:c1], landing, 0, dy, 0, landing))
            for dx in (1, -1):
                depth = HALO - 1 if dx == dy else HALO
                part = span(nx - depth, depth) if dx == 1 else span(0, depth)
                place = span(HALO - depth, depth) if dx == 1 else span(0, depth)
                landing = corner.at[side(dx), side(dy), c0:c1, place]
                waits.append(remote(ysend.at[edge, c0:c1, part], landing, dx, dy, 0, landing))
        return waits, leaving

    def start_slabs(chunk):
        waits = []
        groups_ = slice(2 * chunk, 2 * chunk + 2)
        for dz in (1, 0):
            there_z, here_z = gz, (gz if dz == 0 else 1 - gz)
            for dx in (0, 1, -1):
                for dy in (0, 1, -1):
                    if not (dx or dy or dz):
                        continue
                    edge = 1 if dy == 1 else 0
                    if dx == 0 and dy == 0:
                        src, land = pack.at[groups_], lambda z: packrecv.at[z, groups_]
                    elif dx == 0:
                        src = packedge.at[edge, groups_]
                        land = lambda z, dy=dy: packedgerecv.at[z, side(dy), groups_]
                    elif dy == 0:
                        src = packx.at[side(dx), chunk]
                        land = lambda z, dx=dx: packxrecv.at[z, side(dx), chunk]
                    else:
                        src = packxedge.at[side(dx), edge, chunk]
                        land = lambda z, dx=dx, dy=dy: packxedgerecv.at[z, side(dx), side(dy), chunk]
                    waits.append(remote(src, land(there_z), dx, dy, dz, land(here_z)))
        return waits

    def pack_edges(c0, c1):
        for c in range(c0, c1):
            ysend[0, c] = field[c, own[0], OWNY : OWNY + HALO, :]
            ysend[1, c] = field[c, own[0], OWNY + ny - HALO : OWNY + ny, :]

    lane32 = lax.broadcasted_iota(jnp.int32, (ny, 128), 1)
    quad = lane32 // 4
    upper32 = lax.rem(lane32, 64) >= 32
    lift = 4 * (1 - gz)

    def pack_slab(chunk):
        both = []
        for group in (2 * chunk, 2 * chunk + 1):
            packed = jnp.zeros((ny, 128), F32)
            for part in range(4):
                comp = group * 4 + part
                if comp >= COMPS:
                    continue
                for i in range(nx):
                    base = (part // 2) * 64 + i * 8 + (part % 2) * 4
                    moved = pltpu.roll(field[comp, OWNX + i, own[1], :], base + lift, axis=1)
                    packed = jnp.where(quad == base // 4, moved, packed)
            pack[group] = packed
            packrecv[gz, group] = packed
            packedge[0, group] = packed[0:HALO]
            packedge[1, group] = packed[ny - HALO : ny]
            both.append(packed)
        high = jnp.where(upper32, both[0], pltpu.roll(both[1], 96, axis=1))
        low = jnp.where(upper32, pltpu.roll(both[1], 32, axis=1), both[0])
        for k, value in ((0, high), (1, low)):
            packx[k, chunk] = value
            packxedge[k, 0, chunk] = value[0:HALO]
            packxedge[k, 1, chunk] = value[ny - HALO : ny]

    loads["perm"].wait()
    loads["loss"].wait()
    for i in range(nx):
        loss = medium[1, i]
        field[KEEP, OWNX + i, OWNY : OWNY + ny, :] = (1.0 - loss) / (1.0 + loss)
        field[CURL, OWNX + i, OWNY : OWNY + ny, :] = 0.5 / (medium[0, i] * (1.0 + loss))
    loads["fe"].wait()
    loads["fm"].wait()
    pack_slab(0)
    pack_edges(0, FIRST)
    count_x = 3 - (gx == 0).astype(jnp.int32) - (gx == ngx - 1).astype(jnp.int32)
    count_y = 3 - (gy == 0).astype(jnp.int32) - (gy == ngy - 1).astype(jnp.int32)
    pl.semaphore_wait(barrier, count_x * count_y * 2 - 1 + 30)
    group_start(0, 0, gather1)
    slab_waits = start_slabs(0)
    first_waits, first_leaving = start_halos(
        0, FIRST, ((0, 6, HALO), (KEEP, CURL + 1, HALO - 1)), ((0, 3, HALO), (3, FIRST, HALO - 1))
    )
    loads["ae"].wait()
    loads["am"].wait()
    pack_slab(1)
    pack_edges(FIRST, COMPS)
    loads["source"].wait()
    loads["wave"].wait()
    loads["cells"].wait()
    row = lax.broadcasted_iota(jnp.int32, (ROWS, 128), 0) + TOP
    lane = lax.broadcasted_iota(jnp.int32, (ROWS, 128), 1)
    row_y = row - OWNY + gy * ny
    hrow[...] = jnp.where(row_y >= 0, 0.5, 0.0)
    slab_x = lane // 8 - OWNX + gx * nx
    hslab[...] = jnp.where((row_y >= 0) & (slab_x >= 0), 0.5, 0.0)
    source = source_ref[0]
    total_y, total_z = ngy * ny, ngz * nz
    src_x = source // (total_y * total_z)
    src_y = lax.rem(source // total_z, total_y)
    src_z = lax.rem(source, total_z)
    in_row = row_y == src_y
    smask[...] = jnp.where(in_row & (lane + gz * nz == src_z), 1.0, 0.0)
    slab_z = lax.rem(lane, 8) + nz - HALO
    sslab[...] = jnp.where(in_row & (slab_x == src_x) & (slab_z == src_z), 1.0, 0.0)
    src_plane = src_x - gx * nx + OWNX

    cells = cells_ref[...]
    rec_x = cells // (total_y * total_z) - gx * nx + OWNX
    rec_y = lax.rem(cells // total_z, total_y) - gy * ny + OWNY - TOP
    rec_z = lax.rem(cells, total_z)
    in_x = (rec_x >= 0) & (rec_x < nx + 2 * HALO)
    in_y = (rec_y >= 0) & (rec_y < ROWS)
    rec_row = jnp.where(in_x & in_y, rec_x * ROWS + rec_y, -1)
    rec_lane = rec_z - gz * nz
    planes = nx + 2 * HALO - 2

    def build(i, _):
        ids = lax.broadcasted_iota(jnp.int32, (ROWS, nrec), 0) + (i + 1) * ROWS
        onehot[pl.ds(pl.multiple_of(i * ROWS, 16), ROWS), :] = jnp.where(ids == rec_row, 1.0, 0.0).astype(BF16)
        return 0

    lax.fori_loop(0, planes, build, 0)

    group_wait(0, 0, gather1)
    row_of_samples = gather1[0]
    for k in range(1, 16):
        row_of_samples = row_of_samples + gather1[k]
    gather2[i2] = row_of_samples
    group_start(1, 1, gather2)
    second_slab_waits = start_slabs(1)
    second_waits, second_leaving = start_halos(
        FIRST, COMPS, ((FIRST, COMPS, HALO),), ((8, 11, HALO), (11, COMPS, HALO - 1))
    )

    lane_r = lax.broadcasted_iota(jnp.int32, (ROWS, nz), 1)

    def assemble(c0, c1):
        zeros = jnp.zeros((HALO, nz), F32)
        for c in range(c0, c1):
            for i in range(nx + 2 * HALO):
                for ys in range(2):
                    if i < OWNX:
                        piece = corner[0, ys, c, i]
                    elif i < OWNX + nx:
                        piece = yrecv[ys, c, i - OWNX]
                    else:
                        piece = corner[1, ys, c, i - OWNX - nx]
                    if ys == 0:
                        field[c, i, TOP:OWNY, :] = jnp.concatenate([zeros, piece], axis=0)
                    else:
                        field[c, i, OWNY + ny : OWNY + ny + 8, :] = jnp.concatenate([piece, zeros], axis=0)

    lane_p = lax.broadcasted_iota(jnp.int32, (ROWS, 128), 1)
    deep = lax.rem(lane_p, 8) >= 4
    inside = (lane_p >= 32) & (lane_p < 96)
    upper = lax.rem(lane_p, 64) >= 32

    def assemble_slab(chunk):
        zeros = jnp.zeros((HALO, 128), F32)

        def column(low, middle, high):
            return jnp.concatenate([zeros, low, middle, high, zeros], axis=0)

        sides = [
            [
                column(
                    packxedgerecv[z, k, 0, chunk], packxrecv[z, k, chunk], packxedgerecv[z, k, 1, chunk]
                )
                for k in range(2)
            ]
            for z in range(2)
        ]
        for odd in range(2):
            group = 2 * chunk + odd
            centre, beside = [], []
            for z in range(2):
                centre.append(
                    column(packedgerecv[z, 0, group], packrecv[z, group], packedgerecv[z, 1, group])
                )
                low, high = sides[z]
                if odd:
                    low, high = pltpu.roll(low, 32, axis=1), pltpu.roll(high, 96, axis=1)
                beside.append(jnp.where(upper, low, high))
            for part in range(4):
                comp = group * 4 + part
                if comp >= COMPS:
                    continue
                base = (part // 2) * 64 + (part % 2) * 4
                inner = [pltpu.roll(centre[z], (32 + 4 * z - base) % 128, axis=1) for z in range(2)]
                outer = [pltpu.roll(beside[z], (96 + 4 * z - base) % 128, axis=1) for z in range(2)]
                slab[comp, TOP : TOP + ROWS, :] = jnp.where(
                    inside, jnp.where(deep, inner[1], inner[0]), jnp.where(deep, outer[1], outer[0])
                )

    up_keep = jnp.where(gz == 0, 1.0, 0.0)
    down_keep = jnp.where(gz == 0, 0.0, 1.0)
    def moved(window, by):
        return slice(window.start + by, window.stop + by)

    def magnetic_half(b, step):
        at = slice(TOP, TOP + ROWS) if step < STEPS else slice(TOP, OWNY + ny)
        mask_at = moved(at, -TOP)
        tall = at.stop - at.start
        last_lane = lax.broadcasted_iota(jnp.int32, (tall, nz), 1) == nz - 1
        for i in range(step - 1, nx + 2 * HALO - step):
            factor = hrow[mask_at] * jnp.where(gx * nx + i - OWNX >= 0, 1.0, 0.0)
            ex, ey, ez = field[b, i, at], field[b + 1, i, at], field[b + 2, i, at]
            turn = (nz - 1 - HALO - 8 * i) % 128

            def deeper(value, comp):
                edge = pltpu.roll(slab[comp, at], turn, axis=1) * up_keep
                return jnp.where(last_lane, edge, pltpu.roll(value, nz - 1, axis=1))

            field[b + 3, i, at] = field[b + 3, i, at] - factor * (
                (field[b + 2, i, moved(at, 1)] - ez) - (deeper(ey, b + 1) - ey)
            )
            field[b + 4, i, at] = field[b + 4, i, at] - factor * (
                (deeper(ex, b) - ex) - (field[b + 2, i + 1, at] - ez)
            )
            field[b + 5, i, at] = field[b + 5, i, at] - factor * (
                (field[b + 1, i + 1, at] - ey) - (field[b, i, moved(at, 1)] - ex)
            )
        factor = hslab[mask_at]
        ex, ey, ez = slab[b, at], slab[b + 1, at], slab[b + 2, at]

        def along_x(value):
            return pltpu.roll(value, 120, axis=1)

        def along_z(value):
            return pltpu.roll(value, 127, axis=1)

        slab[b + 3, at] = slab[b + 3, at] - factor * (
            (slab[b + 2, moved(at, 1)] - ez) - (along_z(ey) - ey)
        )
        slab[b + 4, at] = slab[b + 4, at] - factor * ((along_z(ex) - ex) - (along_x(ez) - ez))
        if step < STEPS:
            slab[b + 5, at] = slab[b + 5, at] - factor * (
                (along_x(ey) - ey) - (slab[b, moved(at, 1)] - ex)
            )

    def electric_half(b, step, extra, extra_slab):
        at = slice(TOP, TOP + ROWS) if step < STEPS else own[1]
        tall = at.stop - at.start
        first_lane = lax.broadcasted_iota(jnp.int32, (tall, nz), 1) == 0
        for i in range(step, nx + 2 * HALO - step):
            keep, curl = field[KEEP, i, at], field[CURL, i, at]
            hx, hy, hz = field[b + 3, i, at], field[b + 4, i, at], field[b + 5, i, at]
            turn = (1 - HALO - 8 * i) % 128

            def shallower(value, comp):
                edge = pltpu.roll(slab[comp, at], turn, axis=1) * down_keep
                return jnp.where(first_lane, edge, pltpu.roll(value, 1, axis=1))

            field[b, i, at] = keep * field[b, i, at] + curl * (
                (hz - field[b + 5, i, moved(at, -1)]) - (hy - shallower(hy, b + 4))
            )
            field[b + 1, i, at] = keep * field[b + 1, i, at] + curl * (
                (hx - shallower(hx, b + 3)) - (hz - field[b + 5, i - 1, at])
            )
            field[b + 2, i, at] = (
                keep * field[b + 2, i, at]
                + curl * ((hy - field[b + 4, i - 1, at]) - (hx - field[b + 3, i, moved(at, -1)]))
                + extra(i, moved(at, -TOP))
            )
        if step == STEPS:
            return
        keep, curl = slab[KEEP, at], slab[CURL, at]
        hx, hy, hz = slab[b + 3, at], slab[b + 4, at], slab[b + 5, at]

        def along_x(value):
            return pltpu.roll(value, 8, axis=1)

        def along_z(value):
            return pltpu.roll(value, 1, axis=1)

        slab[b, at] = keep * slab[b, at] + curl * ((hz - slab[b + 5, moved(at, -1)]) - (hy - along_z(hy)))
        slab[b + 1, at] = keep * slab[b + 1, at] + curl * ((hx - along_z(hx)) - (hz - along_x(hz)))
        slab[b + 2, at] = (
            keep * slab[b + 2, at]
            + curl * ((hy - along_x(hy)) - (hx - slab[b + 3, moved(at, -1)]))
            + extra_slab()
        )

    def snapshot(n):
        for c in range(3):
            for i in range(nx):
                value = field[c, OWNX + i, own[1], :]
                if n < STEPS:
                    snaps[n, c, i] = value
                if n:
                    change[n - 1, c, i] = value - snaps[n - 1, c, i]

    for wait in first_waits + slab_waits + first_leaving:
        wait()
    snapshot(0)
    assemble(0, FIRST)
    assemble_slab(0)

    def pulse(step):
        return wave_ref[start + step - 1]

    def forward_electric(step):
        electric_half(
            0,
            step,
            lambda i, at: smask[at] * jnp.where(i == src_plane, pulse(step), 0.0),
            lambda: sslab[...] * pulse(step),
        )
        snapshot(step)

    def split(value):
        high = value.astype(BF16).astype(F32)
        return high, value - high

    contract = (((1,), (1,)), ((), ()))

    def inject(m):
        high, low = split(samples[STEPS - 1 - m])
        weights = jnp.concatenate(
            [jnp.where(at_lane, high, 0.0).astype(BF16), jnp.where(at_lane, low, 0.0).astype(BF16)],
            axis=0,
        )
        count = planes - 2 * m
        both = lax.dot_general(
            onehot[m * ROWS : (m + count) * ROWS, :], weights, contract, preferred_element_type=F32
        )
        inj[m, 1 + m : 1 + m + count] = (both[:, :nz] + both[:, nz:]).reshape(count, ROWS, nz)

    def inject_slab():
        rec_near = rec_x * 8 + rec_z - (nz - HALO)
        in_slab = in_x & (rec_z >= nz - HALO) & (rec_z < nz + HALO)
        slab_weights = jnp.where(lanes_of == jnp.where(in_slab, rec_near, -1), 1.0, 0.0).astype(BF16)
        at_row = lax.broadcasted_iota(jnp.int32, (ROWS, nrec), 0) == rec_y
        pieces = []
        for m in range(STEPS - 1):
            for value in split(samples[STEPS - 1 - m]):
                pieces.append(jnp.where(at_row, value, 0.0).astype(BF16))
        both = lax.dot_general(
            jnp.concatenate(pieces, axis=0), slab_weights, contract, preferred_element_type=F32
        )
        for m in range(STEPS - 1):
            at = 2 * m * ROWS
            injslab[m] = both[at : at + ROWS] + both[at + ROWS : at + 2 * ROWS]

    for step in (1, 2):
        magnetic_half(0, step)
        forward_electric(step)
    group_wait(1, 1, gather2)
    samples = [
        jnp.concatenate([gather2[k][m : m + 1] for k in range(16)], axis=1) for m in range(STEPS)
    ]
    lanes_of = lax.broadcasted_iota(jnp.int32, (nz, nrec), 0)
    at_lane = lanes_of == rec_lane
    inject(0)
    magnetic_half(0, 3)
    inject(1)
    forward_electric(3)
    inject(2)
    magnetic_half(0, 4)
    inject(3)
    inject_slab()
    forward_electric(4)

    for wait in second_waits + second_slab_waits + second_leaving:
        wait()
    assemble(FIRST, COMPS)
    assemble_slab(1)
    for step in range(1, STEPS + 1):
        magnetic_half(FIRST, step)
        electric_half(
            FIRST,
            step,
            lambda i, at, m=step - 1: inj[m, i, at],
            lambda m=step - 1: injslab[m],
        )
        square = jnp.zeros((ny, nz), F32)
        for i in range(nx):
            term = None
            for c in range(3):
                product = change[STEPS - step, c, i] * field[FIRST + c, OWNX + i, own[1], :]
                term = product if term is None else term + product
            value = term if step == 1 else out_ref[i] + term
            if step == STEPS:
                value = -value / medium[0, i]
                square = square + value * value
            out_ref[i] = value
    red1[i1] = jnp.sum(square, axis=0, keepdims=True)
    group_start(2, 0, red1)
    group_wait(2, 0, red1)
    total = red1[0]
    for k in range(1, 16):
        total = total + red1[k]
    red2[i2] = total
    group_start(3, 1, red2)
    group_wait(3, 1, red2)
    total = red2[0]
    for k in range(1, 16):
        total = total + red2[k]
    total = jnp.sum(total, axis=1, keepdims=True)
    cells_in_all = ngx * nx * ngy * ny * ngz * nz
    rms = jnp.sqrt(total / cells_in_all + 1e-06)
    rms_ref[...] = rms
    for cond, copy in sends:
        guarded(cond, copy.wait_send)
    group_drain(0, 0, gather1)
    group_drain(1, 1, gather2)
    group_drain(2, 0, red1)
    group_drain(3, 1, red2)


def solution(mesh):
    ngx, ngy, ngz = mesh.shape["gx"], mesh.shape["gy"], mesh.shape["gz"]

    def per_device(
        permittivity,
        loss,
        fwd_electric,
        fwd_magnetic,
        adj_electric,
        adj_magnetic,
        wavelet,
        residuals,
        source_cell,
        receiver_cells,
        start_step,
    ):
        nx, ny, nz = permittivity.shape
        nrec, trace = receiver_cells.shape[0], residuals.shape[1]
        planes = nx + 2 * HALO
        dims = (ngx, ngy, ngz, nx, ny, nz, nrec)
        hbm = pl.BlockSpec(memory_space=pltpu.HBM)
        vmem = pl.BlockSpec(memory_space=pltpu.VMEM)
        gradient, rms = pl.pallas_call(
            functools.partial(kernel, dims),
            out_shape=(
                jax.ShapeDtypeStruct((nx, ny, nz), F32),
                jax.ShapeDtypeStruct((1, 1), F32),
            ),
            in_specs=[hbm] * 11,
            out_specs=(vmem, vmem),
            scratch_shapes=[
                pltpu.VMEM((COMPS, planes, 64, nz), F32),
                pltpu.VMEM((2, nx, ny, nz), F32),
                pltpu.VMEM((2, COMPS, nx, HALO, nz), F32),
                pltpu.VMEM((2, COMPS, nx, HALO, nz), F32),
                pltpu.VMEM((2, 2, COMPS, HALO, HALO, nz), F32),
                pltpu.VMEM((nrec // (ngx * ngy * ngz), trace), F32),
                pltpu.VMEM((1, nrec), jnp.int32),
                pltpu.SMEM((trace,), F32),
                pltpu.SMEM((1,), jnp.int32),
                pltpu.SMEM((1,), jnp.int32),
                pltpu.VMEM((4, ny, 128), F32),
                pltpu.VMEM((2, 4, HALO, 128), F32),
                pltpu.VMEM((2, 2, ny, 128), F32),
                pltpu.VMEM((2, 2, 2, HALO, 128), F32),
                pltpu.VMEM((2, 4, ny, 128), F32),
                pltpu.VMEM((2, 2, 4, HALO, 128), F32),
                pltpu.VMEM((2, 2, 2, ny, 128), F32),
                pltpu.VMEM((2, 2, 2, 2, HALO, 128), F32),
                pltpu.VMEM((COMPS, 64, 128), F32),
                pltpu.VMEM((STEPS, 3, nx, ny, nz), F32),
                pltpu.VMEM((STEPS, 3, nx, ny, nz), F32),
                pltpu.VMEM((ROWS, 128), F32),
                pltpu.VMEM((ROWS, 128), F32),
                pltpu.VMEM((ROWS, 128), F32),
                pltpu.VMEM((ROWS, 128), F32),
                pltpu.VMEM(((planes - 2) * ROWS, nrec), BF16),
                pltpu.VMEM((STEPS, planes, ROWS, nz), F32),
                pltpu.VMEM((STEPS - 1, ROWS, 128), F32),
                pltpu.VMEM((16, STEPS, 128), F32),
                pltpu.VMEM((16, STEPS, 128), F32),
                pltpu.VMEM((16, 1, 128), F32),
                pltpu.VMEM((16, 1, 128), F32),
                pltpu.SemaphoreType.DMA((11,)),
                pltpu.SemaphoreType.DMA((53,)),
                pltpu.SemaphoreType.DMA((53,)),
                pltpu.SemaphoreType.DMA((4, 15)),
                pltpu.SemaphoreType.DMA((4, 16)),
            ],
            compiler_params=pltpu.CompilerParams(
                collective_id=0, has_side_effects=True, vmem_limit_bytes=60 * 1024 * 1024
            ),
            name="window",
        )(
            permittivity,
            loss,
            fwd_electric,
            fwd_magnetic,
            adj_electric,
            adj_magnetic,
            residuals,
            receiver_cells.reshape(1, nrec),
            wavelet,
            source_cell,
            start_step,
        )
        rms = rms.reshape(())
        return gradient / rms, rms

    field_spec = P(None, "gx", "gy", "gz")
    block_spec = P("gx", "gy", "gz")
    return jax.shard_map(
        per_device,
        mesh=mesh,
        in_specs=(
            block_spec,
            block_spec,
            field_spec,
            field_spec,
            field_spec,
            field_spec,
            P(),
            P(("gx", "gy", "gz"), None),
            P(),
            P(),
            P(),
        ),
        out_specs=(block_spec, P()),
        check_vma=False,
    )
```

time: 70.7 us -> 50.4 us (0.71)
  Pallas kernels: 65.2 us -> 44.2 us
  other arithmetic: 0 us -> 2.26 us
  local copies, waits for them, and re-layouts: 1.57 us -> 0 us
    pallas_call x1, Pallas kernels: 65.2 us -> 44.2 us  [per_device(): pl.pallas_call(functools.partial(kernel, dims), out_shape=(jax.ShapeDtype...]
    div x0 -> x1, other arithmetic: none -> 2.26 us  [per_device(): return (gradient / rms, rms)]
    unnamed x1 -> x0, local copies, waits for them, and re-layouts: 1.57 us -> none
where the time goes in v3:
time: 50.4 us; the launch traced here: 50.2 us
  Pallas kernels  44.2 us (88%)
  between operations  3.74 us (7%)
  other arithmetic  2.26 us (4%)
    pallas_call x1, Pallas kernels, per_device(): pl.pallas_call(functools.partial(kernel, dims), out_shape=(jax.ShapeDtype...  44.2 us
    div x1, other arithmetic, per_device(): return (gradient / rms, rms)  2.26 us

profile of v3, /device:TPU:1, one launch (start us, length us, event | category | flops | bytes accessed | tf_op | source)
XLA Modules:
  0.0 50.2 jit_solution(5313514174289805179)
XLA Ops:
  1.9 44.2 %window.1 = (f32[8,32,128]{2,1,0:T(8,128)}, f32[1,1]{1,0:T(1,128)}) custom-call(f32[8,32,128]{2,1,0:T(8,128)} %perm_hbm.1, f32[8,32,128]{2,1,0:T(8,128)} %loss_hbm.1, f32[3,8,32,128]{3,2,1,0:T(8,128)} %fe_hbm.1, f32[3,8,32,128]{3,2,1,0:T(8,128)} %fm_hbm.1, f32[3,8,32,128]{3,2,1,0:T(8,128)} %ae_hbm.1, f32[3,8,32,128]{3,2,1,0:T(8,128)} %am_hbm.1, ...), custom_call_target="tpu_custom_call" | custom-call | tf_op jit(solution)/shard_map/window/pallas_call | solution.py:709
  46.1 2.3 %broadcast_divide_fusion = f32[8,32,128]{2,1,0:T(8,128)} fusion(f32[8,32,128]{2,1,0:T(8,128)} %get-tuple-element.4, f32[]{:T(128)} %bitcast.1), kind=kLoop, calls=%fused_computation | loop fusion | flops 32768 | bytes 262148 | tf_op jit(solution)/shard_map/div | solution.py:774

commit v4 on v3

--- a/solution.py
+++ b/solution.py
@@ -77,8 +77,6 @@
 ):
     ngx, ngy, ngz, nx, ny, nz, nrec = dims
     gx, gy, gz = lax.axis_index("gx"), lax.axis_index("gy"), lax.axis_index("gz")
-    i1 = lax.rem(gy, 8) * 2 + gz
-    i2 = gx * 2 + gy // 8
     own = (slice(OWNX, OWNX + nx), slice(OWNY, OWNY + ny))
 
     loads = {}
@@ -115,6 +113,55 @@
             fn()
         else:
             pl.when(cond)(fn)
+
+    x_low, z_chip = gy // 8, lax.rem(gy, 8)
+    y_chip, core = gx // 2, lax.rem(gx, 2)
+
+    def device(z, x_hi, y, core, x_lo):
+        return {"gx": y * 2 + core, "gy": x_lo * 8 + z, "gz": x_hi}
+
+    groups = (
+        (z_chip * 2 + gz, lambda k: device(k // 2, lax.rem(k, 2), y_chip, core, x_low)),
+        (gx * 2 + x_low, lambda k: device(z_chip, gz, k // 4, lax.rem(k // 2, 2), lax.rem(k, 2))),
+        (
+            (gz * 2 + x_low) * 4 + y_chip,
+            lambda k: device(z_chip, k // 8, lax.rem(k, 4), core, lax.rem(k // 4, 2)),
+        ),
+        (z_chip * 2 + core, lambda k: device(k // 2, gz, y_chip, lax.rem(k, 2), x_low)),
+    )
+    i1, i2 = groups[0][0], groups[1][0]
+
+    barrier = pltpu.get_barrier_semaphore()
+    apart = sorted(
+        {(dz, dh, 0, 0, 0) for dz in range(8) for dh in range(2)}
+        | {(0, 0, dy, dc, dl) for dy in range(4) for dc in range(2) for dl in range(2)}
+        | {(0, dh, dy, 0, dl) for dh in range(2) for dy in range(4) for dl in range(2)}
+        | {(dz, 0, 0, dc, 0) for dz in range(8) for dc in range(2)}
+    )[1:]
+    for dz, dh, dy, dc, dl in apart:
+        pl.semaphore_signal(
+            barrier,
+            inc=1,
+            device_id=device(
+                lax.rem(z_chip + dz, 8),
+                lax.rem(gz + dh, 2),
+                lax.rem(y_chip + dy, 4),
+                lax.rem(core + dc, 2),
+                lax.rem(x_low + dl, 2),
+            ),
+            device_id_type=MESH,
+        )
+    for dx in (-1, 0, 1):
+        for dy in (-1, 0, 1):
+            for dz in (0, 1):
+                if dx or dy or dz:
+                    peer = {"gx": gx + dx, "gy": gy + dy, "gz": gz if dz == 0 else 1 - gz}
+                    guarded(
+                        there(dx, dy),
+                        lambda peer=peer: pl.semaphore_signal(
+                            barrier, inc=1, device_id=peer, device_id_type=MESH
+                        ),
+                    )
 
     def clear_planes(low):
         def body(c, _):
@@ -152,32 +199,6 @@
         for z in range(2):
             pl.when(missing)(lambda z=z, xs=xs: clear(packxrecv.at[z, xs]))
 
-    barrier = pltpu.get_barrier_semaphore()
-    for dx in (-1, 0, 1):
-        for dy in (-1, 0, 1):
-            for dz in (0, 1):
-                if dx or dy or dz:
-                    peer = {"gx": gx + dx, "gy": gy + dy, "gz": gz if dz == 0 else 1 - gz}
-                    guarded(
-                        there(dx, dy),
-                        lambda peer=peer: pl.semaphore_signal(
-                            barrier, inc=1, device_id=peer, device_id_type=MESH
-                        ),
-                    )
-
-    def member1(k):
-        return {"gx": gx, "gy": (gy // 8) * 8 + k // 2, "gz": lax.rem(k, 2)}
-
-    def member2(k):
-        return {"gx": k // 2, "gy": lax.rem(k, 2) * 8 + lax.rem(gy, 8), "gz": gz}
-
-    groups = ((i1, member1), (i2, member2))
-    for mine, member in groups:
-        for step in range(1, 16):
-            pl.semaphore_signal(
-                barrier, inc=1, device_id=member(lax.rem(mine + step, 16)), device_id_type=MESH
-            )
-
     loads["start"].wait()
     loads["res"].wait()
     start = start_ref[0]
@@ -231,7 +252,7 @@
     sends = []
     number = [0]
 
-    def remote(src, dst, dx, dy, dz, back):
+    def remote(src, dst, dx, dy, dz, back, also=None):
         k = number[0]
         number[0] += 1
 
@@ -245,9 +266,12 @@
                 device_id_type=MESH,
             )
 
-        guarded(there(dx, dy), lambda: make(dst).start())
-        sends.append((there(dx, dy), make(dst)))
-        return lambda: guarded(there(-dx, -dy), lambda: make(back).wait_recv())
+        go, come = there(dx, dy), there(-dx, -dy)
+        if also is not None:
+            go, come = go & also, come & also
+        guarded(go, lambda: make(dst).start())
+        sends.append((go, make(dst)))
+        return lambda: guarded(come, lambda: make(back).wait_recv())
 
     def side(d):
         return 0 if d == 1 else 1
@@ -255,7 +279,7 @@
     def span(low, count):
         return slice(low, low + count)
 
-    def start_halos(c0, c1, low_parts, high_parts):
+    def start_along_x(low_parts, high_parts):
         waits, leaving = [], []
         rows_ = slice(OWNY, OWNY + ny)
         for dx, parts in ((1, low_parts), (-1, high_parts)):
@@ -268,41 +292,65 @@
                 waits.append(remote(field.at[first:last, source, rows_], landing, dx, 0, 0, landing))
                 cond, copy = sends.pop()
                 leaving.append(lambda cond=cond, copy=copy: guarded(cond, copy.wait_send))
+        return waits, leaving
+
+    def start_along_y(c0, c1):
+        waits = []
         for dy in (1, -1):
-            edge = 1 if dy == 1 else 0
             landing = yrecv.at[side(dy), c0:c1]
-            waits.append(remote(ysend.at[edge, c0:c1], landing, 0, dy, 0, landing))
+            waits.append(remote(ysend.at[1 if dy == 1 else 0, c0:c1], landing, 0, dy, 0, landing))
+        return waits
+
+    def relay_corners(c0, c1):
+        waits = []
+        for ys, dy in ((0, -1), (1, 1)):
             for dx in (1, -1):
-                depth = HALO - 1 if dx == dy else HALO
+                depth = HALO - 1 if dx == -dy else HALO
                 part = span(nx - depth, depth) if dx == 1 else span(0, depth)
                 place = span(HALO - depth, depth) if dx == 1 else span(0, depth)
-                landing = corner.at[side(dx), side(dy), c0:c1, place]
-                waits.append(remote(ysend.at[edge, c0:c1, part], landing, dx, dy, 0, landing))
-        return waits, leaving
-
-    def start_slabs(chunk):
+                landing = corner.at[side(dx), ys, c0:c1, place]
+                waits.append(
+                    remote(yrecv.at[ys, c0:c1, part], landing, dx, 0, 0, landing, there(0, dy))
+                )
+        return waits
+
+    def start_along_z(chunk):
+        groups_ = span(2 * chunk, 2)
+        return remote(pack.at[groups_], packrecv.at[gz, groups_], 0, 0, 1, packrecv.at[1 - gz, groups_])
+
+    def start_slabs(chunk, which):
+        z = gz if which == 0 else 1 - gz
         waits = []
-        groups_ = slice(2 * chunk, 2 * chunk + 2)
-        for dz in (1, 0):
-            there_z, here_z = gz, (gz if dz == 0 else 1 - gz)
-            for dx in (0, 1, -1):
-                for dy in (0, 1, -1):
-                    if not (dx or dy or dz):
-                        continue
-                    edge = 1 if dy == 1 else 0
-                    if dx == 0 and dy == 0:
-                        src, land = pack.at[groups_], lambda z: packrecv.at[z, groups_]
-                    elif dx == 0:
-                        src = packedge.at[edge, groups_]
-                        land = lambda z, dy=dy: packedgerecv.at[z, side(dy), groups_]
-                    elif dy == 0:
-                        src = packx.at[side(dx), chunk]
-                        land = lambda z, dx=dx: packxrecv.at[z, side(dx), chunk]
-                    else:
-                        src = packxedge.at[side(dx), edge, chunk]
-                        land = lambda z, dx=dx, dy=dy: packxedgerecv.at[z, side(dx), side(dy), chunk]
-                    waits.append(remote(src, land(there_z), dx, dy, dz, land(here_z)))
+        groups_ = span(2 * chunk, 2)
+        for dx in (0, 1, -1):
+            for dy in (0, 1, -1):
+                if not (dx or dy):
+                    continue
+                edge = 1 if dy == 1 else 0
+                if dx == 0:
+                    src, land = packedge.at[which, edge, groups_], packedgerecv.at[z, side(dy), groups_]
+                elif dy == 0:
+                    src, land = packx.at[which, side(dx), chunk], packxrecv.at[z, side(dx), chunk]
+                else:
+                    src = packxedge.at[which, side(dx), edge, chunk]
+                    land = packxedgerecv.at[z, side(dx), side(dy), chunk]
+                waits.append(remote(src, land, dx, dy, 0, land))
         return waits
+
+    def share_slab(chunk, which, both):
+        for k in range(2):
+            packedge[which, 0, 2 * chunk + k] = both[k][0:HALO]
+            packedge[which, 1, 2 * chunk + k] = both[k][ny - HALO : ny]
+        high = jnp.where(upper32, both[0], pltpu.roll(both[1], 96, axis=1))
+        low = jnp.where(upper32, pltpu.roll(both[1], 32, axis=1), both[0])
+        for k, value in ((0, high), (1, low)):
+            packx[which, k, chunk] = value
+            packxedge[which, k, 0, chunk] = value[0:HALO]
+            packxedge[which, k, 1, chunk] = value[ny - HALO : ny]
+
+    def relay_slabs(chunk):
+        share_slab(chunk, 1, [packrecv[1 - gz, 2 * chunk + k] for k in range(2)])
+        return start_slabs(chunk, 1)
 
     def pack_edges(c0, c1):
         for c in range(c0, c1):
@@ -328,15 +376,8 @@
                     packed = jnp.where(quad == base // 4, moved, packed)
             pack[group] = packed
             packrecv[gz, group] = packed
-            packedge[0, group] = packed[0:HALO]
-            packedge[1, group] = packed[ny - HALO : ny]
             both.append(packed)
-        high = jnp.where(upper32, both[0], pltpu.roll(both[1], 96, axis=1))
-        low = jnp.where(upper32, pltpu.roll(both[1], 32, axis=1), both[0])
-        for k, value in ((0, high), (1, low)):
-            packx[k, chunk] = value
-            packxedge[k, 0, chunk] = value[0:HALO]
-            packxedge[k, 1, chunk] = value[ny - HALO : ny]
+        share_slab(chunk, 0, both)
 
     loads["perm"].wait()
     loads["loss"].wait()
@@ -350,16 +391,22 @@
     pack_edges(0, FIRST)
     count_x = 3 - (gx == 0).astype(jnp.int32) - (gx == ngx - 1).astype(jnp.int32)
     count_y = 3 - (gy == 0).astype(jnp.int32) - (gy == ngy - 1).astype(jnp.int32)
-    pl.semaphore_wait(barrier, count_x * count_y * 2 - 1 + 30)
+    pl.semaphore_wait(barrier, count_x * count_y * 2 - 1 + len(apart))
     group_start(0, 0, gather1)
-    slab_waits = start_slabs(0)
-    first_waits, first_leaving = start_halos(
-        0, FIRST, ((0, 6, HALO), (KEEP, CURL + 1, HALO - 1)), ((0, 3, HALO), (3, FIRST, HALO - 1))
+    first_z = start_along_z(0)
+    first_waits, first_leaving = start_along_x(
+        ((0, 3, HALO), (3, 4, HALO - 1), (4, 6, HALO), (KEEP, CURL + 1, HALO - 1)),
+        ((0, 1, HALO - 1), (1, 3, HALO), (3, FIRST, HALO - 1)),
     )
+    first_y = start_along_y(0, FIRST)
+    first_waits += start_slabs(0, 0)
     loads["ae"].wait()
     loads["am"].wait()
     pack_slab(1)
     pack_edges(FIRST, COMPS)
+    second_z = start_along_z(1)
+    second_y = start_along_y(FIRST, COMPS)
+    second_waits = start_slabs(1, 0)
     loads["source"].wait()
     loads["wave"].wait()
     loads["cells"].wait()
@@ -403,10 +450,16 @@
         row_of_samples = row_of_samples + gather1[k]
     gather2[i2] = row_of_samples
     group_start(1, 1, gather2)
-    second_slab_waits = start_slabs(1)
-    second_waits, second_leaving = start_halos(
-        FIRST, COMPS, ((FIRST, COMPS, HALO),), ((8, 11, HALO), (11, COMPS, HALO - 1))
+    first_z()
+    first_waits += relay_slabs(0)
+    for wait in first_y:
+        wait()
+    first_waits += relay_corners(0, FIRST)
+    second_x, second_leaving = start_along_x(
+        ((8, 11, HALO), (11, 12, HALO - 1), (12, COMPS, HALO)),
+        ((8, 9, HALO - 1), (9, 11, HALO), (11, COMPS, HALO - 1)),
     )
+    second_waits += second_x
 
     lane_r = lax.broadcasted_iota(jnp.int32, (ROWS, nz), 1)
 
@@ -479,7 +532,9 @@
         tall = at.stop - at.start
         last_lane = lax.broadcasted_iota(jnp.int32, (tall, nz), 1) == nz - 1
         for i in range(step - 1, nx + 2 * HALO - step):
-            factor = hrow[mask_at] * jnp.where(gx * nx + i - OWNX >= 0, 1.0, 0.0)
+            factor = hrow[mask_at]
+            if i < OWNX:
+                factor = factor * jnp.where(gx > 0, 1.0, 0.0)
             ex, ey, ez = field[b, i, at], field[b + 1, i, at], field[b + 2, i, at]
             turn = (nz - 1 - HALO - 8 * i) % 128
 
@@ -566,7 +621,7 @@
                 if n:
                     change[n - 1, c, i] = value - snaps[n - 1, c, i]
 
-    for wait in first_waits + slab_waits + first_leaving:
+    for wait in first_waits + first_leaving:
         wait()
     snapshot(0)
     assemble(0, FIRST)
@@ -621,6 +676,11 @@
     for step in (1, 2):
         magnetic_half(0, step)
         forward_electric(step)
+    second_z()
+    second_waits += relay_slabs(1)
+    for wait in second_y:
+        wait()
+    second_waits += relay_corners(FIRST, COMPS)
     group_wait(1, 1, gather2)
     samples = [
         jnp.concatenate([gather2[k][m : m + 1] for k in range(16)], axis=1) for m in range(STEPS)
@@ -637,7 +697,7 @@
     inject_slab()
     forward_electric(4)
 
-    for wait in second_waits + second_slab_waits + second_leaving:
+    for wait in second_waits + second_leaving:
         wait()
     assemble(FIRST, COMPS)
     assemble_slab(1)
@@ -660,15 +720,15 @@
                 value = -value / medium[0, i]
                 square = square + value * value
             out_ref[i] = value
-    red1[i1] = jnp.sum(square, axis=0, keepdims=True)
-    group_start(2, 0, red1)
-    group_wait(2, 0, red1)
+    red1[groups[2][0]] = jnp.sum(square, axis=0, keepdims=True)
+    group_start(2, 2, red1)
+    group_wait(2, 2, red1)
     total = red1[0]
     for k in range(1, 16):
         total = total + red1[k]
-    red2[i2] = total
-    group_start(3, 1, red2)
-    group_wait(3, 1, red2)
+    red2[groups[3][0]] = total
+    group_start(3, 3, red2)
+    group_wait(3, 3, red2)
     total = red2[0]
     for k in range(1, 16):
         total = total + red2[k]
@@ -676,12 +736,15 @@
     cells_in_all = ngx * nx * ngy * ny * ngz * nz
     rms = jnp.sqrt(total / cells_in_all + 1e-06)
     rms_ref[...] = rms
+    wide = jnp.broadcast_to(rms, (ny, nz))
+    for i in range(nx):
+        out_ref[i] = out_ref[i] / wide
     for cond, copy in sends:
         guarded(cond, copy.wait_send)
     group_drain(0, 0, gather1)
     group_drain(1, 1, gather2)
-    group_drain(2, 0, red1)
-    group_drain(3, 1, red2)
+    group_drain(2, 2, red1)
+    group_drain(3, 3, red2)
 
 
 def solution(mesh):
@@ -706,7 +769,7 @@
         dims = (ngx, ngy, ngz, nx, ny, nz, nrec)
         hbm = pl.BlockSpec(memory_space=pltpu.HBM)
         vmem = pl.BlockSpec(memory_space=pltpu.VMEM)
-        gradient, rms = pl.pallas_call(
+        direction, rms = pl.pallas_call(
             functools.partial(kernel, dims),
             out_shape=(
                 jax.ShapeDtypeStruct((nx, ny, nz), F32),
@@ -726,9 +789,9 @@
                 pltpu.SMEM((1,), jnp.int32),
                 pltpu.SMEM((1,), jnp.int32),
                 pltpu.VMEM((4, ny, 128), F32),
-                pltpu.VMEM((2, 4, HALO, 128), F32),
-                pltpu.VMEM((2, 2, ny, 128), F32),
-                pltpu.VMEM((2, 2, 2, HALO, 128), F32),
+                pltpu.VMEM((2, 2, 4, HALO, 128), F32),
+                pltpu.VMEM((2, 2, 2, ny, 128), F32),
+                pltpu.VMEM((2, 2, 2, 2, HALO, 128), F32),
                 pltpu.VMEM((2, 4, ny, 128), F32),
                 pltpu.VMEM((2, 2, 4, HALO, 128), F32),
                 pltpu.VMEM((2, 2, 2, ny, 128), F32),
@@ -748,8 +811,8 @@
                 pltpu.VMEM((16, 1, 128), F32),
                 pltpu.VMEM((16, 1, 128), F32),
                 pltpu.SemaphoreType.DMA((11,)),
-                pltpu.SemaphoreType.DMA((53,)),
-                pltpu.SemaphoreType.DMA((53,)),
+                pltpu.SemaphoreType.DMA((59,)),
+                pltpu.SemaphoreType.DMA((59,)),
                 pltpu.SemaphoreType.DMA((4, 15)),
                 pltpu.SemaphoreType.DMA((4, 16)),
             ],
@@ -770,8 +833,7 @@
             source_cell,
             start_step,
         )
-        rms = rms.reshape(())
-        return gradient / rms, rms
+        return direction, rms.reshape(())
 
     field_spec = P(None, "gx", "gy", "gz")
     block_spec = P("gx", "gy", "gz")

time: 50.4 us -> 49.5 us (0.982)
  other arithmetic: 2.26 us -> 0 us
  local copies, waits for them, and re-layouts: 0 us -> 1.57 us
    div x1 -> x0, other arithmetic: 2.26 us -> none  [per_device(): return (gradient / rms, rms)]
    unnamed x0 -> x1, local copies, waits for them, and re-layouts: none -> 1.57 us
where the time goes in v4:
time: 49.5 us; the launch traced here: 49.4 us
  Pallas kernels  44 us (89%)
  between operations  3.74 us (8%)
  local copies, waits for them, and re-layouts  1.57 us (3%)
    pallas_call x1, Pallas kernels, per_device(): pl.pallas_call(functools.partial(kernel, dims), out_shape=(jax.ShapeDtype...  44 us
    unnamed x1, local copies, waits for them, and re-layouts  1.57 us

profile of v4, /device:TPU:1, one launch (start us, length us, event | category | flops | bytes accessed | tf_op | source)
XLA Modules:
  0.0 49.4 jit_solution(14540962025073292065)
XLA Ops:
  1.9 44.0 %window.1 = (f32[8,32,128]{2,1,0:T(8,128)}, f32[1,1]{1,0:T(1,128)}) custom-call(f32[8,32,128]{2,1,0:T(8,128)} %perm_hbm.1, f32[8,32,128]{2,1,0:T(8,128)} %loss_hbm.1, f32[3,8,32,128]{3,2,1,0:T(8,128)} %fe_hbm.1, f32[3,8,32,128]{3,2,1,0:T(8,128)} %fm_hbm.1, f32[3,8,32,128]{3,2,1,0:T(8,128)} %ae_hbm.1, f32[3,8,32,128]{3,2,1,0:T(8,128)} %am_hbm.1, ...), custom_call_target="tpu_custom_call" | custom-call | tf_op jit(solution)/shard_map/window/pallas_call | solution.py:772
  46.0 1.6 %copy.17 = f32[8,32,128]{2,1,0:T(8,128)} copy(f32[8,32,128]{2,1,0:T(8,128)} %get-tuple-element.8) | data formatting | bytes 262144

commit v5 on v4

--- a/solution.py
+++ b/solution.py
@@ -320,7 +320,7 @@
 
     def start_slabs(chunk, which):
         z = gz if which == 0 else 1 - gz
-        waits = []
+        edges, sides = [], []
         groups_ = span(2 * chunk, 2)
         for dx in (0, 1, -1):
             for dy in (0, 1, -1):
@@ -334,8 +334,8 @@
                 else:
                     src = packxedge.at[which, side(dx), edge, chunk]
                     land = packxedgerecv.at[z, side(dx), side(dy), chunk]
-                waits.append(remote(src, land, dx, dy, 0, land))
-        return waits
+                (sides if dx else edges).append(remote(src, land, dx, dy, 0, land))
+        return edges, sides
 
     def share_slab(chunk, which, both):
         for k in range(2):
@@ -399,14 +399,11 @@
         ((0, 1, HALO - 1), (1, 3, HALO), (3, FIRST, HALO - 1)),
     )
     first_y = start_along_y(0, FIRST)
-    first_waits += start_slabs(0, 0)
+    first_slabs = start_slabs(0, 0)
     loads["ae"].wait()
     loads["am"].wait()
     pack_slab(1)
     pack_edges(FIRST, COMPS)
-    second_z = start_along_z(1)
-    second_y = start_along_y(FIRST, COMPS)
-    second_waits = start_slabs(1, 0)
     loads["source"].wait()
     loads["wave"].wait()
     loads["cells"].wait()
@@ -444,17 +441,23 @@
 
     lax.fori_loop(0, planes, build, 0)
 
+    first_z()
+    first_edges, first_sides = first_slabs
+    edges_, sides_ = relay_slabs(0)
+    first_edges, first_waits = first_edges + edges_, first_waits + first_sides + sides_
+    for wait in first_y:
+        wait()
+    first_waits += relay_corners(0, FIRST)
+
     group_wait(0, 0, gather1)
     row_of_samples = gather1[0]
     for k in range(1, 16):
         row_of_samples = row_of_samples + gather1[k]
     gather2[i2] = row_of_samples
     group_start(1, 1, gather2)
-    first_z()
-    first_waits += relay_slabs(0)
-    for wait in first_y:
-        wait()
-    first_waits += relay_corners(0, FIRST)
+    second_z = start_along_z(1)
+    second_y = start_along_y(FIRST, COMPS)
+    second_edges, second_waits = start_slabs(1, 0)
     second_x, second_leaving = start_along_x(
         ((8, 11, HALO), (11, 12, HALO - 1), (12, COMPS, HALO)),
         ((8, 9, HALO - 1), (9, 11, HALO), (11, COMPS, HALO - 1)),
@@ -463,10 +466,10 @@
 
     lane_r = lax.broadcasted_iota(jnp.int32, (ROWS, nz), 1)
 
-    def assemble(c0, c1):
+    def assemble(c0, c1, planes_):
         zeros = jnp.zeros((HALO, nz), F32)
         for c in range(c0, c1):
-            for i in range(nx + 2 * HALO):
+            for i in planes_:
                 for ys in range(2):
                     if i < OWNX:
                         piece = corner[0, ys, c, i]
@@ -479,18 +482,22 @@
                     else:
                         field[c, i, OWNY + ny : OWNY + ny + 8, :] = jnp.concatenate([piece, zeros], axis=0)
 
+    every = list(range(nx + 2 * HALO))
+    middle = every[OWNX : OWNX + nx]
+    outside = every[:OWNX] + every[OWNX + nx :]
+
     lane_p = lax.broadcasted_iota(jnp.int32, (ROWS, 128), 1)
     deep = lax.rem(lane_p, 8) >= 4
     inside = (lane_p >= 32) & (lane_p < 96)
     upper = lax.rem(lane_p, 64) >= 32
 
-    def assemble_slab(chunk):
+    def assemble_slab(chunk, with_sides=True):
         zeros = jnp.zeros((HALO, 128), F32)
 
         def column(low, middle, high):
             return jnp.concatenate([zeros, low, middle, high, zeros], axis=0)
 
-        sides = [
+        sides = with_sides and [
             [
                 column(
                     packxedgerecv[z, k, 0, chunk], packxrecv[z, k, chunk], packxedgerecv[z, k, 1, chunk]
@@ -506,32 +513,35 @@
                 centre.append(
                     column(packedgerecv[z, 0, group], packrecv[z, group], packedgerecv[z, 1, group])
                 )
-                low, high = sides[z]
-                if odd:
-                    low, high = pltpu.roll(low, 32, axis=1), pltpu.roll(high, 96, axis=1)
-                beside.append(jnp.where(upper, low, high))
+                if with_sides:
+                    low, high = sides[z]
+                    if odd:
+                        low, high = pltpu.roll(low, 32, axis=1), pltpu.roll(high, 96, axis=1)
+                    beside.append(jnp.where(upper, low, high))
             for part in range(4):
                 comp = group * 4 + part
                 if comp >= COMPS:
                     continue
                 base = (part // 2) * 64 + (part % 2) * 4
                 inner = [pltpu.roll(centre[z], (32 + 4 * z - base) % 128, axis=1) for z in range(2)]
-                outer = [pltpu.roll(beside[z], (96 + 4 * z - base) % 128, axis=1) for z in range(2)]
-                slab[comp, TOP : TOP + ROWS, :] = jnp.where(
-                    inside, jnp.where(deep, inner[1], inner[0]), jnp.where(deep, outer[1], outer[0])
-                )
+                near = jnp.where(deep, inner[1], inner[0])
+                far = 0.0
+                if with_sides:
+                    outer = [pltpu.roll(beside[z], (96 + 4 * z - base) % 128, axis=1) for z in range(2)]
+                    far = jnp.where(deep, outer[1], outer[0])
+                slab[comp, TOP : TOP + ROWS, :] = jnp.where(inside, near, far)
 
     up_keep = jnp.where(gz == 0, 1.0, 0.0)
     down_keep = jnp.where(gz == 0, 0.0, 1.0)
     def moved(window, by):
         return slice(window.start + by, window.stop + by)
 
-    def magnetic_half(b, step):
+    def magnetic_half(b, step, planes_):
         at = slice(TOP, TOP + ROWS) if step < STEPS else slice(TOP, OWNY + ny)
         mask_at = moved(at, -TOP)
         tall = at.stop - at.start
         last_lane = lax.broadcasted_iota(jnp.int32, (tall, nz), 1) == nz - 1
-        for i in range(step - 1, nx + 2 * HALO - step):
+        for i in planes_:
             factor = hrow[mask_at]
             if i < OWNX:
                 factor = factor * jnp.where(gx > 0, 1.0, 0.0)
@@ -569,11 +579,11 @@
                 (along_x(ey) - ey) - (slab[b, moved(at, 1)] - ex)
             )
 
-    def electric_half(b, step, extra, extra_slab):
+    def electric_half(b, step, planes_, extra, extra_slab):
         at = slice(TOP, TOP + ROWS) if step < STEPS else own[1]
         tall = at.stop - at.start
         first_lane = lax.broadcasted_iota(jnp.int32, (tall, nz), 1) == 0
-        for i in range(step, nx + 2 * HALO - step):
+        for i in planes_:
             keep, curl = field[KEEP, i, at], field[CURL, i, at]
             hx, hy, hz = field[b + 3, i, at], field[b + 4, i, at], field[b + 5, i, at]
             turn = (1 - HALO - 8 * i) % 128
@@ -612,32 +622,45 @@
             + extra_slab()
         )
 
-    def snapshot(n):
-        for c in range(3):
-            for i in range(nx):
-                value = field[c, OWNX + i, own[1], :]
+    def snapshot(n, planes_):
+        for i in planes_:
+            if i not in middle:
+                continue
+            k = i - OWNX
+            for c in range(3):
+                value = field[c, i, own[1], :]
                 if n < STEPS:
-                    snaps[n, c, i] = value
+                    snaps[n, c, k] = value
                 if n:
-                    change[n - 1, c, i] = value - snaps[n - 1, c, i]
-
-    for wait in first_waits + first_leaving:
+                    change[n - 1, c, k] = value - snaps[n - 1, c, k]
+
+    for wait in first_edges + first_leaving:
         wait()
-    snapshot(0)
-    assemble(0, FIRST)
-    assemble_slab(0)
 
     def pulse(step):
         return wave_ref[start + step - 1]
 
-    def forward_electric(step):
+    def magnetic_planes(step):
+        return every[step - 1 : nx + 2 * HALO - step]
+
+    def electric_planes(step):
+        return every[step : nx + 2 * HALO - step]
+
+    def magnetic_inner(step):
+        return middle[step - 1 : nx - step]
+
+    def electric_inner(step):
+        return middle[step : nx - step]
+
+    def forward_electric(step, planes_):
         electric_half(
             0,
             step,
+            planes_,
             lambda i, at: smask[at] * jnp.where(i == src_plane, pulse(step), 0.0),
             lambda: sslab[...] * pulse(step),
         )
-        snapshot(step)
+        snapshot(step, planes_)
 
     def split(value):
         high = value.astype(BF16).astype(F32)
@@ -673,11 +696,30 @@
             at = 2 * m * ROWS
             injslab[m] = both[at : at + ROWS] + both[at + ROWS : at + 2 * ROWS]
 
+    snapshot(0, middle)
+    assemble(0, FIRST, middle)
+    assemble_slab(0, False)
+    for step in range(1, STEPS + 1):
+        magnetic_half(0, step, magnetic_inner(step))
+        forward_electric(step, electric_inner(step))
+    for wait in first_waits:
+        wait()
+    assemble(0, FIRST, outside)
+    assemble_slab(0)
+
+    def magnetic_outer(step):
+        magnetic_half(0, step, [i for i in magnetic_planes(step) if i not in magnetic_inner(step)])
+
+    def electric_outer(step):
+        forward_electric(step, [i for i in electric_planes(step) if i not in electric_inner(step)])
+
     for step in (1, 2):
-        magnetic_half(0, step)
-        forward_electric(step)
+        magnetic_outer(step)
+        electric_outer(step)
     second_z()
-    second_waits += relay_slabs(1)
+    edges_, sides_ = relay_slabs(1)
+    second_edges += edges_
+    second_waits += sides_
     for wait in second_y:
         wait()
     second_waits += relay_corners(FIRST, COMPS)
@@ -688,38 +730,47 @@
     lanes_of = lax.broadcasted_iota(jnp.int32, (nz, nrec), 0)
     at_lane = lanes_of == rec_lane
     inject(0)
-    magnetic_half(0, 3)
+    magnetic_outer(3)
     inject(1)
-    forward_electric(3)
+    electric_outer(3)
     inject(2)
-    magnetic_half(0, 4)
+    magnetic_outer(4)
     inject(3)
     inject_slab()
-    forward_electric(4)
-
-    for wait in second_waits + second_leaving:
-        wait()
-    assemble(FIRST, COMPS)
-    assemble_slab(1)
-    for step in range(1, STEPS + 1):
-        magnetic_half(FIRST, step)
+    electric_outer(4)
+
+    square = [jnp.zeros((ny, nz), F32)]
+
+    def adjoint_step(step, magnetic_at, electric_at):
+        magnetic_half(FIRST, step, magnetic_at)
         electric_half(
             FIRST,
             step,
-            lambda i, at, m=step - 1: inj[m, i, at],
-            lambda m=step - 1: injslab[m],
-        )
-        square = jnp.zeros((ny, nz), F32)
-        for i in range(nx):
+            electric_at,
+            lambda i, at: inj[step - 1, i, at],
+            lambda: injslab[step - 1],
+        )
+        for i in electric_at:
+            if i not in middle:
+                continue
+            k = i - OWNX
             term = None
             for c in range(3):
-                product = change[STEPS - step, c, i] * field[FIRST + c, OWNX + i, own[1], :]
+                product = change[STEPS - step, c, k] * field[FIRST + c, i, own[1], :]
                 term = product if term is None else term + product
-            value = term if step == 1 else out_ref[i] + term
+            value = term if step == 1 else out_ref[k] + term
             if step == STEPS:
-                value = -value / medium[0, i]
-                square = square + value * value
-            out_ref[i] = value
+                value = -value / medium[0, k]
+                square[0] = square[0] + value * value
+            out_ref[k] = value
+
+    for wait in second_edges + second_waits + second_leaving:
+        wait()
+    assemble(FIRST, COMPS, every)
+    assemble_slab(1)
+    for step in range(1, STEPS + 1):
+        adjoint_step(step, magnetic_planes(step), electric_planes(step))
+    square = square[0]
     red1[groups[2][0]] = jnp.sum(square, axis=0, keepdims=True)
     group_start(2, 2, red1)
     group_wait(2, 2, red1)

time: 49.5 us -> 47.1 us (0.952)
  Pallas kernels: 44 us -> 41.6 us
    pallas_call x1, Pallas kernels: 44 us -> 41.6 us  [per_device(): pl.pallas_call(functools.partial(kernel, dims), out_shape=(jax.ShapeDtype...]
where the time goes in v5:
time: 47.1 us; the launch traced here: 47 us
  Pallas kernels  41.6 us (88%)
  between operations  3.74 us (8%)
  local copies, waits for them, and re-layouts  1.57 us (3%)
    pallas_call x1, Pallas kernels, per_device(): pl.pallas_call(functools.partial(kernel, dims), out_shape=(jax.ShapeDtype...  41.6 us
    unnamed x1, local copies, waits for them, and re-layouts  1.57 us

profile of v5, /device:TPU:1, one launch (start us, length us, event | category | flops | bytes accessed | tf_op | source)
XLA Modules:
  0.0 47.0 jit_solution(1275161065708200586)
XLA Ops:
  1.9 41.6 %window.1 = (f32[8,32,128]{2,1,0:T(8,128)}, f32[1,1]{1,0:T(1,128)}) custom-call(f32[8,32,128]{2,1,0:T(8,128)} %perm_hbm.1, f32[8,32,128]{2,1,0:T(8,128)} %loss_hbm.1, f32[3,8,32,128]{3,2,1,0:T(8,128)} %fe_hbm.1, f32[3,8,32,128]{3,2,1,0:T(8,128)} %fm_hbm.1, f32[3,8,32,128]{3,2,1,0:T(8,128)} %ae_hbm.1, f32[3,8,32,128]{3,2,1,0:T(8,128)} %am_hbm.1, ...), custom_call_target="tpu_custom_call" | custom-call | tf_op jit(solution)/shard_map/window/pallas_call | solution.py:823
  43.6 1.6 %copy.17 = f32[8,32,128]{2,1,0:T(8,128)} copy(f32[8,32,128]{2,1,0:T(8,128)} %get-tuple-element.8) | data formatting | bytes 262144

commit v6 on v5

--- a/solution.py
+++ b/solution.py
@@ -130,6 +130,13 @@
         (z_chip * 2 + core, lambda k: device(k // 2, gz, y_chip, lax.rem(k, 2), x_low)),
     )
     i1, i2 = groups[0][0], groups[1][0]
+    hops = (
+        lambda k: min(k // 2, 8 - k // 2) + 2 * (k % 2),
+        lambda k: min(k // 4, 4 - k // 4) + k % 2,
+        lambda k: min(k // 4, 4 - k // 4) + min(k % 4, 4 - k % 4),
+        lambda k: min(k // 2, 8 - k // 2),
+    )
+    orders = [sorted(range(1, 16), key=lambda k, far=far: -far(k)) for far in hops]
 
     barrier = pltpu.get_barrier_semaphore()
     apart = sorted(
@@ -138,6 +145,7 @@
         | {(0, dh, dy, 0, dl) for dh in range(2) for dy in range(4) for dl in range(2)}
         | {(dz, 0, 0, dc, 0) for dz in range(8) for dc in range(2)}
     )[1:]
+    apart.sort(key=lambda o: -(min(o[0], 8 - o[0]) + 2 * o[1] + min(o[2], 4 - o[2]) + o[4]))
     for dz, dh, dy, dc, dl in apart:
         pl.semaphore_signal(
             barrier,
@@ -238,7 +246,7 @@
         )
 
     def group_start(round_, which, ref):
-        for step in range(1, 16):
+        for step in orders[which]:
             group_copy(round_, which, ref, step).start()
 
     def group_wait(round_, which, ref):
@@ -372,7 +380,8 @@
                     continue
                 for i in range(nx):
                     base = (part // 2) * 64 + i * 8 + (part % 2) * 4
-                    moved = pltpu.roll(field[comp, OWNX + i, own[1], :], base + lift, axis=1)
+                    turn = lax.rem(base + lift, 128)
+                    moved = pltpu.roll(field[comp, OWNX + i, own[1], :], turn, axis=1)
                     packed = jnp.where(quad == base // 4, moved, packed)
             pack[group] = packed
             packrecv[gz, group] = packed

time: 47.1 us -> 47.2 us (level)
  no operation moved by 1% of the time
where the time goes in v6:
time: 47.2 us; the launch traced here: 47 us
  Pallas kernels  41.7 us (88%)
  between operations  3.74 us (8%)
  local copies, waits for them, and re-layouts  1.57 us (3%)
    pallas_call x1, Pallas kernels, per_device(): pl.pallas_call(functools.partial(kernel, dims), out_shape=(jax.ShapeDtype...  41.7 us
    unnamed x1, local copies, waits for them, and re-layouts  1.57 us

profile of v6, /device:TPU:1, one launch (start us, length us, event | category | flops | bytes accessed | tf_op | source)
XLA Modules:
  0.0 47.0 jit_solution(2004111003014340323)
XLA Ops:
  1.9 41.7 %window.1 = (f32[8,32,128]{2,1,0:T(8,128)}, f32[1,1]{1,0:T(1,128)}) custom-call(f32[8,32,128]{2,1,0:T(8,128)} %perm_hbm.1, f32[8,32,128]{2,1,0:T(8,128)} %loss_hbm.1, f32[3,8,32,128]{3,2,1,0:T(8,128)} %fe_hbm.1, f32[3,8,32,128]{3,2,1,0:T(8,128)} %fm_hbm.1, f32[3,8,32,128]{3,2,1,0:T(8,128)} %ae_hbm.1, f32[3,8,32,128]{3,2,1,0:T(8,128)} %am_hbm.1, ...), custom_call_target="tpu_custom_call" | custom-call | tf_op jit(solution)/shard_map/window/pallas_call | solution.py:832
  43.6 1.6 %copy.17 = f32[8,32,128]{2,1,0:T(8,128)} copy(f32[8,32,128]{2,1,0:T(8,128)} %get-tuple-element.8) | data formatting | bytes 262144
